TPU v7x, 256 devices: a whole 4x4x8 slice. The times are simulated.
256 devices in a mesh: grp: 32 (over z, y), rep: 8 (over x, core).
Axes of the slice: x: 4, y: 4, z: 8, core: 2. Of those that a mesh axis runs over, the one named last changes fastest.
Arguments:
- queries: bfloat16 [64, 8, 32, 128], P('grp', 'rep'), may hold values from -3.2 to 3.2
- passages: bfloat16 [2048, 8, 180, 128], P('grp', 'rep'), may hold values from -1.796875 to 1.796875
- lengths: int32 [2048, 8], P('grp', 'rep'), may hold values from 16 to 180
- cand_ids: int32 [64, 8, 64], P('grp', 'rep'), may hold values from 0 to 2047, as said below
- owner_map: int32 [8, 2048], P('rep'), may hold values from 0 to 2047, as said below
- teacher: float32 [64, 8, 64], P('grp', 'rep'), may hold values from -12 to 312
- weights: float32 [64, 8], P('grp', 'rep'), may hold values from 0.5 to 18
Outputs:
- loss: float32 [], replicated
- query_grad: float32 [64, 8, 32, 128], P('grp', 'rep')
- passage_grad: bfloat16 [2048, 8, 180, 128], P('grp', 'rep')
Inputs may be any that keep to these rules, and one draw needn't show every extreme that they name: `cand_ids`: within each replica, the 128 candidates of the queries of one grp index have storage rows of which at most 8 (counted with repeats) lie in any one aligned block of 64 rows; in every draw, in each replica, one block receives exactly 8 from every grp index. `owner_map`: each row is a permutation of 0 to 2047.
All inputs are finite; a program needn't handle non-finite values.
Results may differ from a plain program's by a relative error of at most 0.0055.
Values may be sent and summed in bfloat16 or wider, within the bound.
A program may use at most 128 MiB of HBM per device.

v0:
```python
import jax
import jax.numpy as jnp
from jax import lax
from jax.sharding import Mesh
from jax.sharding import PartitionSpec as P

GRP = ("grp_0", "grp_1")
REP = ("rep_0", "rep_1")
GRP_REP = ("grp_0", "grp_1", "rep_0", "rep_1")


temper = 0.05


def over_axes(shard, axes):
    for axis in axes:
        shard = lax.psum(shard, axis)
    return shard


def token_softmax(products, lengths_used):
    usable = (
        lax.broadcasted_iota(jnp.int32, products.shape, products.ndim - 1)
        < lengths_used[..., None, None]
    )
    scaled = jnp.where(usable, products / temper, -1e30)
    highest = jnp.max(scaled, axis=-1, keepdims=True)
    powers = jnp.where(usable, jnp.exp(scaled - highest), 0.0)
    summed = jnp.sum(powers, axis=-1, keepdims=True)
    matched = temper * (highest[..., 0] + jnp.log(summed[..., 0]))
    return (matched, powers / summed)


def on_device(queries, passages, lengths, cand_ids, owner_map, teacher, weights):
    groups = lax.axis_size(GRP)
    replicas = lax.axis_size(REP)
    query_local = queries.shape[0]
    query_len = queries.shape[2]
    feature_dim = queries.shape[3]
    passage_local = passages.shape[0]
    token_len = passages.shape[2]
    candidates = cand_ids.shape[2]
    ref_count = query_local * candidates
    capacity = 2 * ref_count // groups
    slot_count = groups * capacity
    block_width = token_len * feature_dim
    query_width = query_len * feature_dim
    position_table = owner_map[0]
    wanted = cand_ids[:, 0, :].reshape(ref_count)
    table_index = jnp.arange(position_table.shape[0], dtype=jnp.int32)
    positions = jnp.sum(
        jnp.where(wanted[:, None] == table_index[None, :], position_table[None, :], 0), axis=1
    )
    owner_index = positions // passage_local
    local_row = positions % passage_local
    owner_hot = (owner_index[:, None] == jnp.arange(groups, dtype=jnp.int32)[None, :]).astype(
        jnp.int32
    )
    before = jnp.cumsum(owner_hot, axis=0) - owner_hot
    slot_rank = jnp.sum(before * owner_hot, axis=1)
    slot_index = owner_index * capacity + slot_rank
    request = jnp.full((slot_count,), -1, jnp.int32).at[slot_index].set(local_row)
    asked_rows = lax.all_to_all(
        request.reshape(groups, capacity), GRP, split_axis=0, concat_axis=0, tiled=True
    ).reshape(slot_count)
    present = asked_rows >= 0
    safe_rows = jnp.maximum(asked_rows, 0)
    slot_lengths = jnp.where(present, lengths[:, 0][safe_rows], 0)
    stored_index = jnp.arange(passage_local, dtype=jnp.int32)
    gather_hot = (asked_rows[None, :] == stored_index[:, None]).astype(jnp.bfloat16)
    pick_hot = (asked_rows[:, None] == stored_index[None, :]).astype(jnp.bfloat16)
    route_hot = (slot_index[:, None] == jnp.arange(slot_count, dtype=jnp.int32)[None, :]).astype(
        jnp.bfloat16
    )
    flat_passages = passages.reshape(passage_local, block_width)
    query_flat = queries[:, 0]
    query_weights = weights[:, 0]
    query_source = jnp.arange(ref_count, dtype=jnp.int32) // candidates
    blocks_flat = jnp.dot(pick_hot, flat_passages, preferred_element_type=jnp.float32).astype(
        jnp.bfloat16
    )
    ref_queries = query_flat[query_source].reshape(ref_count, query_width)
    slot_queries = jnp.einsum(
        "rs,rk->sk", route_hot, ref_queries, preferred_element_type=jnp.float32
    ).astype(jnp.bfloat16)
    got_queries = lax.all_to_all(
        slot_queries.reshape(groups, capacity, query_width),
        GRP,
        split_axis=0,
        concat_axis=0,
        tiled=True,
    )
    got_queries = got_queries.reshape(slot_count, query_len, feature_dim)
    blocks = blocks_flat.reshape(slot_count, token_len, feature_dim)
    products = jnp.einsum("sid,sjd->sij", got_queries, blocks, preferred_element_type=jnp.float32)
    matched, attention = token_softmax(products, jnp.maximum(slot_lengths, 1))
    slot_scores = jnp.sum(matched, axis=-1)
    back_scores = lax.all_to_all(
        slot_scores.reshape(groups, capacity), GRP, split_axis=0, concat_axis=0, tiled=True
    ).reshape(slot_count)
    student = back_scores[slot_index].reshape(query_local, candidates)
    log_student = jax.nn.log_softmax(student, axis=-1)
    log_teacher = jax.nn.log_softmax(teacher[:, 0], axis=-1)
    teacher_prob = jnp.exp(log_teacher)
    divergence = jnp.sum(teacher_prob * (log_teacher - log_student), axis=-1)
    totals = (
        over_axes(jnp.sum(query_weights * divergence), GRP_REP),
        over_axes(jnp.sum(query_weights), GRP_REP),
    )
    loss_value = totals[0] / totals[1]
    scale_all = query_local * groups * replicas
    score_grad = (
        scale_all * query_weights[:, None] / totals[1] * (jnp.exp(log_student) - teacher_prob)
    )
    loss_value, score_grad = (loss_value, score_grad)
    slot_score_grad = (
        jnp.zeros((slot_count,), jnp.float32).at[slot_index].set(score_grad.reshape(ref_count))
    )
    arrived = lax.all_to_all(
        slot_score_grad.reshape(groups, capacity), GRP, split_axis=0, concat_axis=0, tiled=True
    ).reshape(slot_count)
    scaled_grad = (arrived[:, None, None] * attention).astype(jnp.bfloat16)
    pair_query = jnp.einsum(
        "sij,sjd->sid", scaled_grad, blocks, preferred_element_type=jnp.float32
    ).astype(jnp.bfloat16)
    returned_queries = lax.all_to_all(
        pair_query.reshape(groups, capacity, query_width),
        GRP,
        split_axis=0,
        concat_axis=0,
        tiled=True,
    )
    ordered = jnp.dot(
        route_hot,
        returned_queries.reshape(slot_count, query_width),
        preferred_element_type=jnp.float32,
    )
    query_grad = jnp.sum(ordered.reshape(query_local, candidates, query_len, feature_dim), axis=1)
    returned = jnp.einsum(
        "sij,sid->sjd", scaled_grad, got_queries, preferred_element_type=jnp.float32
    ).astype(jnp.bfloat16)
    returned = returned.reshape(slot_count, block_width)
    passage_sum = jnp.dot(gather_hot, returned, preferred_element_type=jnp.float32)
    passage_grad = passage_sum.astype(jnp.bfloat16).reshape(
        passage_local, 1, token_len, feature_dim
    )
    return (loss_value, query_grad[:, None], passage_grad)


def solution(mesh):
    finer = Mesh(mesh.devices.reshape(8, 4, 4, 2), ("grp_0", "grp_1", "rep_0", "rep_1"))
    in_specs = (
        P(GRP, REP, None, None),
        P(GRP, REP, None, None),
        P(GRP, REP),
        P(GRP, REP, None),
        P(REP, None),
        P(GRP, REP, None),
        P(GRP, REP),
    )
    out_specs = (P(), P(GRP, REP, None, None), P(GRP, REP, None, None))
    return jax.shard_map(
        on_device, mesh=finer, in_specs=in_specs, out_specs=out_specs, check_vma=False
    )
```

profile of v0, /device:TPU:2, one launch (start us, length us, event | category | flops | bytes accessed | tf_op | source)
XLA Modules:
  0.0 254.9 jit_solution(11497343918002270158)
XLA Ops:
  1.2 1.3 reduce.17
  5.7 11.5 %all-to-all-start = ((s32[32,1,8]{2,1,0:T(1,128)}), s32[32,1,8]{2,1,0:T(1,128)S(1)}, u32[]{:S(2)}, u32[]{:S(2)}) async-start(s32[32,1,8]{2,1,0:T(1,128)} %bitcast.6), calls=%async_computation | async-start | bytes 32768 | tf_op jit(solution)/shard_map/all_to_all | solution.py:63
  18.1 2.2 fusion.1
  20.2 6.7 %all-to-all-done = s32[32,1,8]{2,1,0:T(1,128)S(1)} async-done(((s32[32,1,8]{2,1,0:T(1,128)}), s32[32,1,8]{2,1,0:T(1,128)S(1)}, u32[]{:S(2)}, u32[]{:S(2)}) %all-to-all-start) | async-done | bytes 1056 | tf_op jit(solution)/shard_map/all_to_all | solution.py:63
  26.9 4.9 %all-to-all-start.1 = ((bf16[32,8,4096]{2,1,0:T(8,128)(2,1)}), bf16[32,8,4096]{2,1,0:T(8,128)(2,1)}, u32[]{:S(2)}, u32[]{:S(2)}) async-start(bf16[32,8,4096]{2,1,0:T(8,128)(2,1)} %fusion.1), calls=%async_computation.1 | async-start | bytes 4194304 | tf_op jit(solution)/shard_map/all_to_all | solution.py:86
  31.9 3.7 %copy.30 = bf16[64,1,180,128]{3,2,0,1:T(8,128)(2,1)S(1)} copy(bf16[64,1,180,128]{3,0,2,1:T(8,128)(2,1)} %param.9) | data formatting | bytes 5898240 | tf_op args[1]
  36.8 6.2 %convolution_convert_fusion = bf16[256,23040]{1,0:T(8,128)(2,1)} fusion(bf16[8,8,180,128]{3,2,1,0:T(8,128)(2,1)S(1)} %bitcast.71, s32[256]{0:T(256)S(1)} %reshape.239), kind=kOutput, calls=%fused_computation.5 | convolution fusion | flops 760889344 | bytes 14746624 | tf_op jit(solution)/shard_map/dot_general | solution.py:79
  43.0 16.2 %copy.31 = bf16[256,23040]{0,1:T(8,128)(2,1)} copy(bf16[256,23040]{1,0:T(8,128)(2,1)} %convolution_convert_fusion) | data formatting | bytes 23592960 | tf_op jit(solution)/shard_map/convert_element_type | solution.py:79
  59.3 16.5 %copy.32 = bf16[256,180,128]{2,1,0:T(8,128)(2,1)} copy(bf16[256,180,128]{0,2,1:T(8,128)(2,1)} %bitcast.70) | data formatting | bytes 23592960 | tf_op jit(solution)/shard_map/reshape | solution.py:94
  75.8 1.9 gather_fusion
  77.7 2.2 all-to-all-done.1
  79.9 2.1 copy.41
  82.0 15.2 %fusion = (f32[256,32]{1,0:T(8,128)S(1)}, f32[256,32,180]{2,1,0:T(8,128)}) fusion(s32[256]{0:T(256)S(1)} %fusion.14, bf16[256,32,128]{2,1,0:T(8,128)(2,1)S(1)} %bitcast.73, bf16[256,180,128]{2,1,0:T(8,128)(2,1)} %copy.32), kind=kOutput, calls=%fused_computation.12 | convolution fusion | flops 383377408 | bytes 19825664 | tf_op jit(solution)/shard_map/sid,sjd->sij/dot_general | solution.py:95
  97.2 6.4 %fusion.2 = f32[256,32]{1,0:T(8,128)S(1)} fusion(f32[256,32,180]{2,1,0:T(8,128)} %get-tuple-element.29, f32[256,32]{1,0:T(8,128)S(1)} %get-tuple-element.28, s32[256]{0:T(256)S(1)} %fusion.14), kind=kLoop, calls=%fused_computation.15 | loop fusion | flops 8839168 | bytes 5964800 | tf_op jit(solution)/shard_map/reduce_sum | solution.py:29
  104.5 7.4 %all-to-all-start.2 = ((f32[32,1,8]{2,1,0:T(1,128)}), f32[32,1,8]{2,1,0:T(1,128)S(1)}, u32[]{:S(2)}, u32[]{:S(2)}) async-start(f32[32,1,8]{2,1,0:T(1,128)} %bitcast.12), calls=%async_computation.2 | async-start | bytes 32768 | tf_op jit(solution)/shard_map/all_to_all | solution.py:98
  112.5 9.1 %all-to-all-done.2 = f32[32,1,8]{2,1,0:T(1,128)S(1)} async-done(((f32[32,1,8]{2,1,0:T(1,128)}), f32[32,1,8]{2,1,0:T(1,128)S(1)}, u32[]{:S(2)}, u32[]{:S(2)}) %all-to-all-start.2) | async-done | bytes 1056 | tf_op jit(solution)/shard_map/all_to_all | solution.py:98
  125.3 15.4 %all-reduce = (f32[]{:T(128)}, f32[]{:T(128)}) all-reduce(f32[]{:T(128)} %fusion.17, f32[]{:T(128)} %reduce_sum.97), channel_id=1, replica_groups=mesh['grp_0'=8,'grp_1'=4,'rep_0'=4,'rep_1'=2] {'grp_0'}, use_global_device_ids=true, to_apply=%region_11.13 | all-reduce | flops 2 | bytes 16 | tf_op jit(solution)/shard_map/psum | solution.py:17
  140.7 9.5 %all-reduce.2 = (f32[]{:T(128)}, f32[]{:T(128)}) all-reduce(f32[]{:T(128)} %get-tuple-element.18, f32[]{:T(128)} %get-tuple-element.19), channel_id=1, replica_groups=mesh['grp_0'=8,'grp_1'=4,'rep_0'=4,'rep_1'=2] {'grp_1'}, use_global_device_ids=true, to_apply=%region_12.14 | all-reduce | flops 2 | bytes 16 | tf_op jit(solution)/shard_map/psum | solution.py:17
  150.2 9.2 %all-reduce.1 = (f32[]{:T(128)}, f32[]{:T(128)}) all-reduce(f32[]{:T(128)} %get-tuple-element.22, f32[]{:T(128)} %get-tuple-element.23), channel_id=1, replica_groups=mesh['grp_0'=8,'grp_1'=4,'rep_0'=4,'rep_1'=2] {'rep_0'}, use_global_device_ids=true, to_apply=%region_13.15 | all-reduce | flops 2 | bytes 16 | tf_op jit(solution)/shard_map/psum | solution.py:17
  159.5 3.4 %all-reduce.3 = (f32[]{:T(128)}, f32[]{:T(128)}) all-reduce(f32[]{:T(128)} %get-tuple-element.20, f32[]{:T(128)} %get-tuple-element.21), channel_id=1, replica_groups=mesh['grp_0'=8,'grp_1'=4,'rep_0'=4,'rep_1'=2] {'rep_1'}, use_global_device_ids=true, to_apply=%region_14.16 | all-reduce | flops 2 | bytes 16 | tf_op jit(solution)/shard_map/psum | solution.py:17
  164.8 14.2 %all_to_all.37 = f32[32,1,8]{2,1,0:T(1,128)S(1)} all-to-all(f32[32,1,8]{2,1,0:T(1,128)S(1)} %bitcast.76), channel_id=1, replica_groups=mesh['grp_0'=8,'grp_1'=4,'rep_0'=4,'rep_1'=2] {'grp_0','grp_1'}, dimensions={0} | all-to-all | bytes 2048 | tf_op jit(solution)/shard_map/all_to_all | solution.py:119
  179.8 10.3 %convolution_convert_fusion.4 = bf16[256,32,128]{2,1,0:T(8,128)(2,1)} fusion(bf16[256,180,128]{2,1,0:T(8,128)(2,1)} %copy.32, f32[256,32,180]{2,1,0:T(8,128)} %get-tuple-element.29, f32[256,32]{1,0:T(8,128)S(1)} %fusion.2, f32[256]{0:T(256)S(1)} %mul.78, f32[256,32]{1,0:T(8,128)S(1)} %get-tuple-element.28, s32[256]{0:T(256)S(1)} %fusion.14), kind=kOutput, calls=%fused_computation.18 | convolution fusion | flops 390332416 | bytes 19859456 | tf_op jit(solution)/shard_map/sij,sjd->sid/dot_general | solution.py:123
  190.1 4.2 %reshape.248 = bf16[32,8,4096]{2,1,0:T(8,128)(2,1)} reshape(bf16[256,32,128]{2,1,0:T(8,128)(2,1)} %convolution_convert_fusion.4) | data formatting | bytes 4194304 | tf_op jit(solution)/shard_map/reshape | solution.py:127
  194.3 4.8 %all-to-all-start.4 = ((bf16[32,8,4096]{2,1,0:T(8,128)(2,1)}), bf16[32,8,4096]{2,1,0:T(8,128)(2,1)}, u32[]{:S(2)}, u32[]{:S(2)}) async-start(bf16[32,8,4096]{2,1,0:T(8,128)(2,1)} %reshape.248), calls=%async_computation.4 | async-start | bytes 4194304 | tf_op jit(solution)/shard_map/all_to_all | solution.py:126
  200.6 14.7 %convolution_convert_fusion.2 = bf16[256,180,128]{2,1,0:T(8,128)(2,1)} fusion(bf16[256,32,128]{2,1,0:T(8,128)(2,1)S(1)} %bitcast.74, f32[256,32,180]{2,1,0:T(8,128)} %get-tuple-element.29, f32[256,32]{1,0:T(8,128)S(1)} %fusion.2, f32[256]{0:T(256)S(1)} %mul.78, f32[256,32]{1,0:T(8,128)S(1)} %get-tuple-element.28, s32[256]{0:T(256)S(1)} %fusion.14), kind=kOutput, calls=%fused_computation.11 | convolution fusion | flops 395182080 | bytes 19859456 | tf_op jit(solution)/shard_map/sij,sid->sjd/dot_general | solution.py:139
  215.3 16.4 %copy.37 = bf16[256,180,128]{0,2,1:T(8,128)(2,1)} copy(bf16[256,180,128]{2,1,0:T(8,128)(2,1)} %convolution_convert_fusion.2) | data formatting | bytes 23592960 | tf_op jit(solution)/shard_map/convert_element_type | solution.py:141
  231.7 8.0 %convolution_convert_fusion.1 = bf16[64,23040]{1,0:T(8,128)(2,1)S(1)} fusion(bf16[256,23040]{0,1:T(8,128)(2,1)} %bitcast.69, s32[256]{0:T(256)S(1)} %reshape.239), kind=kOutput, calls=%fused_computation.6 | convolution fusion | flops 756465664 | bytes 14746624 | tf_op jit(solution)/shard_map/dot_general | solution.py:143
  239.7 2.9 %reshape.251 = bf16[64,1,180,128]{3,2,0,1:T(8,128)(2,1)} reshape(bf16[64,23040]{1,0:T(8,128)(2,1)S(1)} %convolution_convert_fusion.1) | data formatting | bytes 5898240 | tf_op jit(solution)/shard_map/reshape | solution.py:144
  242.6 4.2 %copy.38 = bf16[64,1,180,128]{3,0,2,1:T(8,128)(2,1)} copy(bf16[64,1,180,128]{3,2,0,1:T(8,128)(2,1)} %reshape.251) | data formatting | bytes 5898240
  246.8 2.2 all-to-all-done.4
  249.0 3.3 %copy.36 = bf16[256,4096]{0,1:T(8,128)(2,1)S(1)} copy(bf16[256,4096]{1,0:T(8,128)(2,1)} %bitcast.18) | data formatting | bytes 4194304 | tf_op jit(solution)/shard_map/reshape | solution.py:135
  252.3 1.4 convolution_reduce_fusion
  (56 shorter events, 13.8 us)
Async XLA Ops:
  0.6 16.6 %copy-start = (bf16[2,1,32,128]{3,2,1,0:T(8,128)(2,1)S(1)}, bf16[2,1,32,128]{3,2,1,0:T(8,128)(2,1)}, u32[]{:S(2)}) copy-start(bf16[2,1,32,128]{3,2,1,0:T(8,128)(2,1)} %param.8) | copy-start | bytes 49156
  0.6 35.0 %copy-start.3 = (f32[2,1,64]{2,1,0:T(1,128)S(1)}, f32[2,1,64]{2,1,0:T(1,128)}, u32[]{:S(2)}) copy-start(f32[2,1,64]{2,1,0:T(1,128)} %param.13) | copy-start | bytes 1540
  5.7 21.2 %all-to-all-start = ((s32[32,1,8]{2,1,0:T(1,128)}), s32[32,1,8]{2,1,0:T(1,128)S(1)}, u32[]{:S(2)}, u32[]{:S(2)}) async-start(s32[32,1,8]{2,1,0:T(1,128)} %bitcast.6), calls=%async_computation | async-start | bytes 32768 | tf_op jit(solution)/shard_map/all_to_all | solution.py:63
  26.9 53.0 %all-to-all-start.1 = ((bf16[32,8,4096]{2,1,0:T(8,128)(2,1)}), bf16[32,8,4096]{2,1,0:T(8,128)(2,1)}, u32[]{:S(2)}, u32[]{:S(2)}) async-start(bf16[32,8,4096]{2,1,0:T(8,128)(2,1)} %fusion.1), calls=%async_computation.1 | async-start | bytes 4194304 | tf_op jit(solution)/shard_map/all_to_all | solution.py:86
  59.3 16.5 %copy-start.2 = (s32[64,1]{0,1:T(1,128)S(1)}, s32[64,1]{0,1:T(1,128)}, u32[]{:S(2)}) copy-start(s32[64,1]{0,1:T(1,128)} %param.10) | copy-start | bytes 772
  97.2 14.7 %copy-start.4 = (f32[2,1]{0,1:T(1,128)S(1)}, f32[2,1]{0,1:T(1,128)}, u32[]{:S(2)}) copy-start(f32[2,1]{0,1:T(1,128)} %param.14) | copy-start | bytes 28
  104.5 17.1 %all-to-all-start.2 = ((f32[32,1,8]{2,1,0:T(1,128)}), f32[32,1,8]{2,1,0:T(1,128)S(1)}, u32[]{:S(2)}, u32[]{:S(2)}) async-start(f32[32,1,8]{2,1,0:T(1,128)} %bitcast.12), calls=%async_computation.2 | async-start | bytes 32768 | tf_op jit(solution)/shard_map/all_to_all | solution.py:98
  194.3 54.8 %all-to-all-start.4 = ((bf16[32,8,4096]{2,1,0:T(8,128)(2,1)}), bf16[32,8,4096]{2,1,0:T(8,128)(2,1)}, u32[]{:S(2)}, u32[]{:S(2)}) async-start(bf16[32,8,4096]{2,1,0:T(8,128)(2,1)} %reshape.248), calls=%async_computation.4 | async-start | bytes 4194304 | tf_op jit(solution)/shard_map/all_to_all | solution.py:126
  231.7 22.1 %copy-start.1 = (bf16[2,1,32,128]{3,2,1,0:T(8,128)(2,1)S(1)}, bf16[2,1,32,128]{3,2,1,0:T(8,128)(2,1)}, u32[]{:S(2)}) copy-start(bf16[2,1,32,128]{3,2,1,0:T(8,128)(2,1)} %param.8) | copy-start | bytes 49156
where the time goes:
time: 259 us; the launch traced here: 255 us
  local copies, waits for them, and re-layouts  78.7 us (30%)
  matrix products  58 us (22%)
  blocking collectives  51.8 us (20%)
  starting transfers between devices  28.5 us (11%)
  waiting for transfers between devices  20.2 us (8%)
  other arithmetic  14.3 us (6%)
  between operations  3.42 us (1%)
    psum x4, blocking collectives, over_axes(): shard = lax.psum(shard, axis)  37.5 us
    reshape x1, local copies, waits for them, and re-layouts, on_device(): blocks = blocks_flat.reshape(slot_count, token_len, feature_dim)  16.5 us
    convert_element_type x1, local copies, waits for them, and re-layouts, on_device(): returned = jnp.einsum('sij,sid->sjd', scaled_grad, got_queries, preferred...  16.4 us
    convert_element_type x1, local copies, waits for them, and re-layouts, on_device(): jnp.dot(pick_hot, flat_passages, preferred_element_type=jnp.float32)  16.2 us
    dot_general x1, matrix products, on_device(): jnp.einsum('sid,sjd->sij', got_queries, blocks, preferred_element_type=jn...  15.2 us
    dot_general x1, matrix products, on_device(): jnp.einsum('sij,sid->sjd', scaled_grad, got_queries, preferred_element_ty...  14.7 us
    all_to_all x1, blocking collectives, on_device(): lax.all_to_all(slot_score_grad.reshape(groups, capacity), GRP, split_axis...  14.2 us
    all_to_all x1, starting transfers between devices, on_device(): lax.all_to_all(request.reshape(groups, capacity), GRP, split_axis=0, conc...  11.5 us
  transfers between devices with their start and end apart: 4, of which 4 were waited for; matrix products, arithmetic and copies ran while one was open for 38% of the time, Pallas kernels for 0%

commit v1 on v0

v1 whole, which is shorter than its diff:
```python
import functools

import jax
import jax.numpy as jnp
from jax import lax
from jax.experimental import pallas as pl
from jax.experimental.pallas import tpu as pltpu
from jax.sharding import PartitionSpec as P

MESH = pl.DeviceIdType.MESH
F32 = jnp.float32
BF16 = jnp.bfloat16
I32 = jnp.int32

temper = 0.05
SCALE2 = 20.0 * 1.4426950408889634
LANES = 128
CAP = 8
WIDE = 4
UNROLL = 8


def iota(shape, axis):
    return lax.broadcasted_iota(I32, shape, axis)


def to_row(col):
    n = col.shape[0]
    eye = iota((n, n), 0) == iota((n, n), 1)
    return jnp.sum(jnp.where(eye, col, jnp.zeros_like(col)), axis=0, keepdims=True)


def to_col(row):
    n = row.shape[1]
    eye = iota((n, n), 0) == iota((n, n), 1)
    return jnp.sum(jnp.where(eye, row, jnp.zeros_like(row)), axis=1, keepdims=True)


def pick(mask, values):
    return jnp.sum(jnp.where(mask, values, jnp.zeros_like(values)), axis=1, keepdims=True)


def step_kernel(
    G,
    R,
    NCH,
    cand_ref,
    omap_ref,
    q_ref,
    p_hbm,
    len_ref,
    teach_ref,
    w_ref,
    loss_ref,
    qgrad_ref,
    pgrad_hbm,
    p_v,
    q_all,
    x_s,
    y_r,
    v_s,
    v_r,
    g_r,
    wr,
    lr,
    meta_v,
    meta_s,
    m_v,
    att,
    u_v,
    slotr,
    loccol,
    sgq,
    sgl,
    qg_s,
    qg_r,
    acc,
    p_sem,
    meta_sem,
    out_sem,
    y_send,
    y_recv,
    q_send,
    q_recv,
    v_send,
    v_recv,
    g_send,
    g_recv,
    o_send,
    o_recv,
    w_send,
    w_recv,
    l_send,
    l_recv,
):
    me = lax.axis_index("grp")
    rep = lax.axis_index("rep")
    stored, token_len, dim = p_v.shape
    query_len = q_ref.shape[1]
    nslot = G * CAP

    def remote(src, dst, ssem, rsem, g, r):
        return pltpu.make_async_remote_copy(
            src_ref=src,
            dst_ref=dst,
            send_sem=ssem,
            recv_sem=rsem,
            device_id=(g, r),
            device_id_type=MESH,
        )

    def peers(body):
        def one(t, carry):
            body(lax.rem(me + t, G))
            return carry

        lax.fori_loop(1, G, one, 0)

    def reps(body):
        for t in range(1, R):
            body(lax.rem(rep + t, R))

    barrier = pltpu.get_barrier_semaphore()

    def greet(g):
        pl.semaphore_signal(barrier, inc=1, device_id=(g, rep), device_id_type=MESH)

    def greet_rep(r):
        pl.semaphore_signal(barrier, inc=1, device_id=(me, r), device_id_type=MESH)

    peers(greet)
    reps(greet_rep)
    p_copy = pltpu.make_async_copy(p_hbm, p_v, p_sem)
    p_copy.start()

    omap = omap_ref[...]
    count = omap.shape[1]
    wanted = to_col(cand_ref[...])
    pos = pick(wanted == iota((LANES, count), 1), jnp.broadcast_to(omap, (LANES, count)))
    pos_row = to_row(pos)
    owner = pos_row >> 6
    row1 = (pos_row & 63) + 1
    weights = w_ref[...]
    lane = iota((1, LANES), 1)
    half = lane >> 6
    mine_w = pick((lane & 63) == 0, weights)
    x_s[:, 0, :] = jnp.where(owner == iota((G, LANES), 0), row1, 0).astype(F32)
    x_s[:, 1, :] = jnp.broadcast_to(mine_w, (G, LANES))
    q_all[pl.ds(2 * me, 2)] = q_ref[...]
    y_r[me] = x_s[me]

    pl.semaphore_wait(barrier, G - 1 + R - 1)

    def send_y(g):
        remote(x_s.at[g], y_r.at[me], y_send.at[g], y_recv.at[me], g, rep).start()

    def send_q(g):
        remote(
            q_ref, q_all.at[pl.ds(2 * me, 2)], q_send.at[g], q_recv.at[me], g, rep
        ).start()

    peers(send_y)
    peers(send_q)

    def wait_y(g):
        remote(x_s.at[g], y_r.at[g], y_send.at[g], y_recv.at[g], g, rep).wait_recv()

    def wait_q(g):
        remote(
            q_ref, q_all.at[pl.ds(2 * g, 2)], q_send.at[g], q_recv.at[g], g, rep
        ).wait_recv()

    peers(wait_y)

    group_w = jnp.sum(y_r[:, 1, :], axis=0, keepdims=True)
    wr[rep] = group_w

    def send_w(r):
        remote(wr.at[rep], wr.at[rep], w_send.at[r], w_recv.at[rep], me, r).start()

    reps(send_w)

    y = y_r[:, 0, :].astype(I32)
    have = y > 0
    lower = (iota((LANES, LANES), 0) < iota((LANES, LANES), 1)).astype(BF16)
    before = jnp.dot(have.astype(F32).astype(BF16), lower, preferred_element_type=F32).astype(I32)
    ylane = iota((G, LANES), 1)
    code = jnp.where(have, (y << 7) | ylane, 0)
    codes = [pick(have & (before == k), code) for k in range(CAP)]
    for k in range(CAP):
        rk = jnp.where(codes[k] > 0, codes[k] & 127, -1)
        slotr[k] = jnp.broadcast_to(rk, (G, LANES))
    ecode = jnp.concatenate(codes, axis=0)
    ew = ecode >> 7
    er = ecode & 127
    es = jnp.concatenate([iota((G, 1), 0)] * CAP, axis=0)
    ew_row = to_row(ew)
    used_row = ew_row > 0
    same = (ew == ew_row) & used_row
    rank = jnp.sum(
        jnp.where(same & (iota((nslot, nslot), 1) < iota((nslot, nslot), 0)), 1, 0),
        axis=1,
        keepdims=True,
    )
    rank_row = to_row(rank)
    starts = used_row & ((rank_row & (WIDE - 1)) == 0) & (ew_row < ew)
    base = jnp.sum(jnp.where(starts, 1, 0), axis=1, keepdims=True)
    loc = jnp.where(ew > 0, (base + (rank >> 2)) * WIDE + (rank & (WIDE - 1)), -1)
    loccol[...] = jnp.broadcast_to(loc, (nslot, LANES))
    packed = (ew << 12) | (es << 7) | er
    for b in range(WIDE):
        hit = loc == iota((nslot, LANES), 1) * WIDE + b
        meta_v[b : b + 1, :] = jnp.sum(jnp.where(hit, packed, 0), axis=0, keepdims=True)
    loc_row = to_row(loc)
    for h in range(nslot // LANES):
        meta_v[WIDE + h : WIDE + h + 1, :] = loc_row[:, h * LANES : (h + 1) * LANES]
    plane = iota((nslot, LANES), 1) + 1
    begin = (ew > 0) & ((rank & (WIDE - 1)) == 0)
    first = jnp.sum(jnp.where(begin & (ew < plane), 1, 0), axis=0, keepdims=True)
    held = jnp.sum(jnp.where(begin & (ew == plane), 1, 0), axis=0, keepdims=True)
    meta_v[6:7, :] = jnp.where(held > 0, first + 1, 0)
    meta_v[7:8, :] = jnp.zeros((1, LANES), I32)
    meta_copy = pltpu.make_async_copy(meta_v, meta_s, meta_sem)
    meta_copy.start()
    m_v[...] = jnp.zeros_like(m_v)
    meta_copy.wait()
    p_copy.wait()
    peers(wait_q)

    def query_of(b, ch):
        return q_all[(meta_s[b, ch] >> 6) & (2 * G - 1)]

    def passage_of(ch):
        return jnp.maximum((meta_s[0, ch] >> 12) - 1, 0)

    token = iota((token_len, LANES), 0)

    def forward(ch):
        pid = passage_of(ch)
        queries = jnp.concatenate([query_of(b, ch) for b in range(WIDE)], axis=0)
        x = lax.dot_general(
            p_v[pid], queries, (((1,), (1,)), ((), ())), preferred_element_type=F32
        )
        x = jnp.where(token < len_ref[0, pid], x, -1e30)
        highest = jnp.max(x, axis=0, keepdims=True)
        powers = jnp.exp2((x - highest) * SCALE2)
        summed = jnp.sum(powers, axis=0, keepdims=True)
        att[ch] = (powers * (1.0 / summed)).astype(BF16)
        return highest + temper * jnp.log(summed)

    def forward_group(g, carry):
        rows = [forward(g * UNROLL + u) for u in range(UNROLL)]
        m_v[pl.ds(pl.multiple_of(g * UNROLL, UNROLL), UNROLL), :] = jnp.concatenate(rows, axis=0)
        return carry

    lax.fori_loop(0, NCH // UNROLL, forward_group, 0)

    matched = m_v[...]
    block = iota((LANES, LANES), 1) >> 5
    loc_cols = loccol[...]
    scores = jnp.zeros((nslot, 1), F32)
    for b in range(WIDE):
        row = to_row(pick(block == b, matched))
        hit = loc_cols == iota((nslot, LANES), 1) * WIDE + b
        scores += pick(hit, jnp.broadcast_to(row, (nslot, LANES)))
    score_rows = jnp.zeros((G, LANES), F32)
    for k in range(CAP):
        score_rows += jnp.where(slotr[k] == ylane, scores[k * G : (k + 1) * G, :], 0.0)
    v_s[:, 0, :] = score_rows
    v_r[me] = v_s[me]

    def send_v(g):
        remote(v_s.at[g], v_r.at[me], v_send.at[g], v_recv.at[me], g, rep).start()

    peers(send_v)

    def lift(ch):
        u = lax.dot_general(
            att[ch], p_v[passage_of(ch)], (((0,), (0,)), ((), ())), preferred_element_type=F32
        )
        u_v[pl.ds(ch * WIDE, WIDE)] = u.astype(BF16).reshape(WIDE, query_len, dim)

    def lift_group(g, carry):
        for u in range(UNROLL):
            lift(g * UNROLL + u)
        return carry

    lax.fori_loop(0, NCH // UNROLL, lift_group, 0)

    def wait_v(g):
        remote(v_s.at[g], v_r.at[g], v_send.at[g], v_recv.at[g], g, rep).wait_recv()

    def wait_w(r):
        remote(wr.at[r], wr.at[r], w_send.at[r], w_recv.at[r], me, r).wait_recv()

    peers(wait_v)
    reps(wait_w)

    def log_softmax(values):
        top = [jnp.max(jnp.where(half == h, values, -3e38), axis=1, keepdims=True) for h in (0, 1)]
        shifted = values - jnp.where(half == 0, top[0], top[1])
        e = jnp.exp(shifted)
        total = [pick(half == h, e) for h in (0, 1)]
        return shifted - jnp.log(jnp.where(half == 0, total[0], total[1]))

    log_student = log_softmax(jnp.sum(v_r[...], axis=0))
    log_teacher = log_softmax(teach_ref[...])
    teacher_prob = jnp.exp(log_teacher)
    weight_sum = jnp.sum(wr[...], axis=0)
    scale_all = 2.0 * G * R
    score_grad = scale_all * weights / weight_sum * (jnp.exp(log_student) - teacher_prob)
    part = jnp.sum(
        weights * (teacher_prob * (log_teacher - log_student)), axis=1, keepdims=True
    )
    g_r[me] = jnp.concatenate([score_grad, jnp.broadcast_to(part, (1, LANES))], axis=0)

    def send_g(g):
        remote(g_r.at[me], g_r.at[me], g_send.at[g], g_recv.at[me], g, rep).start()

    def wait_g(g):
        remote(g_r.at[g], g_r.at[g], g_send.at[g], g_recv.at[g], g, rep).wait_recv()

    peers(send_g)
    peers(wait_g)

    lr[rep] = jnp.sum(g_r[:, 1, :], axis=0, keepdims=True)

    def send_l(r):
        remote(lr.at[rep], lr.at[rep], l_send.at[r], l_recv.at[rep], me, r).start()

    reps(send_l)

    grads = g_r[:, 0, :]
    by_slot = []
    for k in range(CAP):
        rk = slotr[k]
        col = pick(rk == ylane, grads)
        by_slot.append(col)
        sgq[:, k, :] = jnp.where(rk < 64, col, 0.0)
        sgq[:, CAP + k, :] = jnp.where(rk >= 64, col, 0.0)

    def query_sum(s):
        scales = sgq[s]
        one = jnp.zeros((query_len, dim), F32)
        two = jnp.zeros((query_len, dim), F32)
        for k in range(CAP):
            e = k * G + s
            at = jnp.maximum(meta_s[WIDE + e // LANES, lax.rem(e, LANES)], 0)
            u = u_v[at].astype(F32)
            one += scales[k : k + 1, :] * u
            two += scales[CAP + k : CAP + k + 1, :] * u
        return one.astype(BF16), two.astype(BF16)

    def send_qg(t, carry):
        s = lax.rem(me + t, G)
        one, two = query_sum(s)
        qg_s[s, 0] = one
        qg_s[s, 1] = two
        remote(qg_s.at[s], qg_r.at[me], o_send.at[s], o_recv.at[me], s, rep).start()
        return carry

    lax.fori_loop(1, G, send_qg, 0)
    one, two = query_sum(me)
    qg_r[me, 0] = one
    qg_r[me, 1] = two

    sg_row = to_row(jnp.concatenate(by_slot, axis=0))
    loc_rows = jnp.concatenate(
        [meta_v[WIDE + h : WIDE + h + 1, :] for h in range(nslot // LANES)], axis=1
    )
    for b in range(WIDE):
        hit = loc_rows == iota((LANES, nslot), 0) * WIDE + b
        col = pick(hit, jnp.broadcast_to(sg_row, (LANES, nslot)))
        sgl[:, b, :] = jnp.broadcast_to(col, (LANES, LANES))

    acc[...] = jnp.zeros_like(acc)

    def back(ch):
        scales = sgl[ch]
        scaled = jnp.concatenate(
            [
                (query_of(b, ch).astype(F32) * scales[b : b + 1, :]).astype(BF16)
                for b in range(WIDE)
            ],
            axis=0,
        )
        product = jnp.dot(att[ch], scaled, preferred_element_type=F32)
        follows = (meta_s[0, ch] >> 12) == (meta_s[0, ch + 1] >> 12)
        total = product + acc[...] * jnp.where(follows, 1.0, 0.0)
        acc[...] = total
        att[ch] = total.astype(BF16)

    def back_group(i, carry):
        g = NCH // UNROLL - 1 - i
        for u in range(UNROLL):
            back(g * UNROLL + UNROLL - 1 - u)
        return carry

    lax.fori_loop(0, NCH // UNROLL, back_group, 0)

    def place(p, carry):
        mark = meta_s[6, p]
        p_v[p] = att[jnp.maximum(mark - 1, 0)] * jnp.where(mark > 0, 1.0, 0.0).astype(BF16)
        return carry

    lax.fori_loop(0, stored, place, 0)
    out_copy = pltpu.make_async_copy(p_v, pgrad_hbm, out_sem)
    out_copy.start()

    def wait_l(r):
        remote(lr.at[r], lr.at[r], l_send.at[r], l_recv.at[r], me, r).wait_recv()

    reps(wait_l)
    loss_ref[...] = jnp.sum(lr[...], axis=0) / weight_sum

    def wait_o(g):
        remote(qg_s.at[g], qg_r.at[g], o_send.at[g], o_recv.at[g], g, rep).wait_recv()

    peers(wait_o)

    def add(o, carry):
        return carry + qg_r[o].astype(F32)

    qgrad_ref[...] = lax.fori_loop(0, G, add, jnp.zeros(qgrad_ref.shape, F32))

    def drain(g):
        remote(x_s.at[g], y_r.at[g], y_send.at[g], y_recv.at[g], g, rep).wait_send()
        remote(q_ref, q_all.at[pl.ds(2 * g, 2)], q_send.at[g], q_recv.at[g], g, rep).wait_send()
        remote(v_s.at[g], v_r.at[g], v_send.at[g], v_recv.at[g], g, rep).wait_send()
        remote(g_r.at[g], g_r.at[g], g_send.at[g], g_recv.at[g], g, rep).wait_send()
        remote(qg_s.at[g], qg_r.at[g], o_send.at[g], o_recv.at[g], g, rep).wait_send()

    def drain_rep(r):
        remote(wr.at[r], wr.at[r], w_send.at[r], w_recv.at[r], me, r).wait_send()
        remote(lr.at[r], lr.at[r], l_send.at[r], l_recv.at[r], me, r).wait_send()

    peers(drain)
    reps(drain_rep)
    out_copy.wait()


def on_device(G, R, queries, passages, lengths, cand_ids, owner_map, teacher, weights):
    query_local, _, query_len, dim = queries.shape
    stored, _, token_len, _ = passages.shape
    chunks = (G * CAP + (WIDE - 1) * stored) // WIDE
    NCH = -(-chunks // UNROLL) * UNROLL
    vmem = pl.BlockSpec(memory_space=pltpu.VMEM)
    smem = pl.BlockSpec(memory_space=pltpu.SMEM)
    hbm = pl.BlockSpec(memory_space=pl.ANY)
    dma = pltpu.SemaphoreType.DMA
    shape = jax.ShapeDtypeStruct
    loss, qgrad, pgrad = pl.pallas_call(
        functools.partial(step_kernel, G, R, NCH),
        out_shape=(
            shape((1, LANES), F32),
            shape((query_local, query_len, dim), F32),
            shape((stored, token_len, dim), BF16),
        ),
        in_specs=[vmem, vmem, vmem, hbm, smem, vmem, vmem],
        out_specs=(vmem, vmem, hbm),
        scratch_shapes=[
            pltpu.VMEM((stored, token_len, dim), BF16),
            pltpu.VMEM((query_local * G, query_len, dim), BF16),
            pltpu.VMEM((G, 2, LANES), F32),
            pltpu.VMEM((G, 2, LANES), F32),
            pltpu.VMEM((G, 1, LANES), F32),
            pltpu.VMEM((G, 1, LANES), F32),
            pltpu.VMEM((G, 2, LANES), F32),
            pltpu.VMEM((R, 1, LANES), F32),
            pltpu.VMEM((R, 1, LANES), F32),
            pltpu.VMEM((8, LANES), I32),
            pltpu.SMEM((8, LANES), I32),
            pltpu.VMEM((LANES, LANES), F32),
            pltpu.VMEM((NCH, token_len, LANES), BF16),
            pltpu.VMEM((NCH * WIDE, query_len, dim), BF16),
            pltpu.VMEM((CAP, G, LANES), I32),
            pltpu.VMEM((G * CAP, LANES), I32),
            pltpu.VMEM((G, 2 * CAP, LANES), F32),
            pltpu.VMEM((LANES, WIDE, LANES), F32),
            pltpu.VMEM((G, query_local, query_len, dim), BF16),
            pltpu.VMEM((G, query_local, query_len, dim), BF16),
            pltpu.VMEM((token_len, dim), F32),
            dma,
            dma,
            dma,
        ]
        + [dma((G,))] * 10
        + [dma((R,))] * 4,
        compiler_params=pltpu.CompilerParams(
            collective_id=0, has_side_effects=True, vmem_limit_bytes=56 * 1024 * 1024
        ),
    )(
        cand_ids.reshape(1, LANES),
        owner_map,
        queries.reshape(query_local, query_len, dim),
        passages.reshape(stored, token_len, dim),
        lengths.reshape(1, stored),
        teacher.reshape(1, LANES),
        jnp.repeat(weights.reshape(query_local), LANES // query_local).reshape(1, LANES),
    )
    return loss[0, 0], qgrad[:, None], pgrad[:, None]


def solution(mesh):
    G, R = mesh.shape["grp"], mesh.shape["rep"]
    in_specs = (
        P("grp", "rep", None, None),
        P("grp", "rep", None, None),
        P("grp", "rep"),
        P("grp", "rep", None),
        P("rep", None),
        P("grp", "rep", None),
        P("grp", "rep"),
    )
    out_specs = (P(), P("grp", "rep", None, None), P("grp", "rep", None, None))
    return jax.shard_map(
        functools.partial(on_device, G, R),
        mesh=mesh,
        in_specs=in_specs,
        out_specs=out_specs,
        check_vma=False,
    )
```

time: 259 us -> 81.1 us (0.31); the launches traced: 255 us -> 80.5 us
  local copies, waits for them, and re-layouts: 78.7 us -> 13.7 us
  Pallas kernels: 0 us -> 62.3 us
  matrix products: 58 us -> 0 us
  blocking collectives: 51.8 us -> 0 us
  starting transfers between devices: 28.5 us -> 0 us
  waiting for transfers between devices: 20.2 us -> 0 us
  other arithmetic: 14.3 us -> 2.68 us
    pallas_call x0 -> x1, Pallas kernels: none -> 62.3 us  [on_device(): pl.pallas_call(functools.partial(step_kernel, G, R, NCH), out_shape=(shap...]
    dot_general x7 -> x0, matrix products: 58 us -> none  [the longest x1 15.2 us: on_device(): jnp.einsum('sid,sjd->sij', got_queries, blocks, preferred_element_type=jn...]
    psum x4 -> x0, blocking collectives: 37.5 us -> none  [over_axes(): shard = lax.psum(shard, axis)]
    convert_element_type x2 -> x0, local copies, waits for them, and re-layouts: 32.7 us -> none  [the longest x1 16.4 us: on_device(): returned = jnp.einsum('sij,sid->sjd', scaled_grad, got_queries, preferred...]
    all_to_all x4 -> x0, starting transfers between devices: 28.5 us -> none  [the longest x1 11.5 us: on_device(): lax.all_to_all(request.reshape(groups, capacity), GRP, split_axis=0, conc...]
    reshape x8 -> x2, local copies, waits for them, and re-layouts: 27.2 us -> 1.19 us  [the longest x1 0.59 us: on_device(): cand_ids.reshape(1, LANES)]
    all_to_all x4 -> x0, waiting for transfers between devices: 20.2 us -> none  [the longest x1 9.08 us: on_device(): lax.all_to_all(slot_scores.reshape(groups, capacity), GRP, split_axis=0,...]
    all_to_all x1 -> x0, blocking collectives: 14.2 us -> none  [on_device(): lax.all_to_all(slot_score_grad.reshape(groups, capacity), GRP, split_axis...]
  transfers between devices with their start and end apart: 4 -> 0, of which waited for: 4 -> 0; matrix products, arithmetic and copies ran while one was open for 38% -> 0% of each run, Pallas kernels for 0% -> 0%
where the time goes in v1:
time: 81.1 us; the launch traced here: 80.5 us
  Pallas kernels  62.3 us (77%)
  local copies, waits for them, and re-layouts  13.7 us (17%)
  other arithmetic  2.68 us (3%)
  between operations  1.84 us (2%)
    pallas_call x1, Pallas kernels, on_device(): pl.pallas_call(functools.partial(step_kernel, G, R, NCH), out_shape=(shap...  62.3 us
    unnamed x9, local copies, waits for them, and re-layouts  11.2 us
    unnamed x2, other arithmetic  2.68 us

profile of v1, /device:TPU:2, one launch (start us, length us, event | category | flops | bytes accessed | tf_op | source)
XLA Modules:
  0.0 80.5 jit_solution(5032044763067737177)
XLA Ops:
  0.6 0.5 broadcast.6
  1.1 1.3 %reduce.6 = s32[2,64]{1,0:T(2,128)S(1)} reduce(s32[2,1,64]{2,1,0:T(1,128)} %param.10, s32[]{:T(128)} %broadcast.6), dimensions={1}, to_apply=%param.10.reduce_sub_computation.3 | reduce | bytes 1028 | tf_op args[3]
  2.5 0.6 reshape.24.cand_ref
  3.1 0.5 broadcast.7
  3.6 1.3 %reduce.7 = f32[2,64]{1,0:T(2,128)S(1)} reduce(f32[2,1,64]{2,1,0:T(1,128)} %param.12, f32[]{:T(128)} %broadcast.7), dimensions={1}, to_apply=%param.12.reduce_sub_computation.3 | reduce | bytes 1028 | tf_op args[5]
  4.9 0.6 reshape.28.teach_ref
  5.5 0.7 broadcast_in_dim.9
  6.2 0.6 reshape_reshape.3.w_ref
  6.8 5.4 %copy.14 = bf16[64,1,180,128]{3,2,0,1:T(8,128)(2,1)} copy(bf16[64,1,180,128]{3,0,2,1:T(8,128)(2,1)} %param.8) | data formatting | bytes 5898240 | tf_op args[1]
  12.2 62.3 %shard_map.94 = (f32[1,128]{1,0:T(1,128)}, f32[2,32,128]{2,1,0:T(8,128)}, bf16[64,180,128]{2,1,0:T(8,128)(2,1)}) custom-call(s32[1,128]{1,0:T(1,128)} %reshape.24.cand_ref, s32[1,2048]{1,0:T(1,128)} %omap_ref.1, bf16[2,32,128]{2,1,0:T(8,128)(2,1)} %bitcast.15, bf16[64,180,128]{2,1,0:T(8,128)(2,1)} %bitcast.12, s32[1,64]{1,0:T(1,128)} %bitcast.16, ...), custom_call_target="tpu_custom_call" | custom-call | tf_op jit(solution)/shard_map/pallas_call | solution.py:452
  74.5 0.0 copy-start.1
  74.5 0.0 copy-start
  74.5 4.2 %copy.12 = bf16[64,1,180,128]{3,0,2,1:T(8,128)(2,1)} copy(bf16[64,1,180,128]{3,2,0,1:T(8,128)(2,1)} %bitcast.13) | data formatting | bytes 5898240
  78.7 0.0 copy-done.1
  78.8 0.0 copy-done
  78.8 0.6 copy.18
Async XLA Ops:
  74.5 4.3 %copy-start.1 = (f32[1,128]{1,0:T(1,128)S(1)}, f32[1,128]{1,0:T(1,128)}, u32[]{:S(2)}) copy-start(f32[1,128]{1,0:T(1,128)} %get-tuple-element.6) | copy-start | bytes 1540
  74.5 4.3 %copy-start = (f32[2,32,128]{2,1,0:T(8,128)S(1)}, f32[2,32,128]{2,1,0:T(8,128)}, u32[]{:S(2)}) copy-start(f32[2,32,128]{2,1,0:T(8,128)} %get-tuple-element.7) | copy-start | bytes 98308

commit v2 on v1

--- a/solution.py
+++ b/solution.py
@@ -18,6 +18,7 @@
 CAP = 8
 WIDE = 4
 UNROLL = 8
+LOW = -3e38
 
 
 def iota(shape, axis):
@@ -53,12 +54,15 @@
     w_ref,
     loss_ref,
     qgrad_ref,
-    pgrad_hbm,
+    pgrad_ref,
+    pt_v,
+    p_f,
     p_v,
     q_all,
+    c_v,
     x_s,
     y_r,
-    v_s,
+    t_r,
     v_r,
     g_r,
     wr,
@@ -77,11 +81,12 @@
     acc,
     p_sem,
     meta_sem,
-    out_sem,
     y_send,
     y_recv,
     q_send,
     q_recv,
+    t_send,
+    t_recv,
     v_send,
     v_recv,
     g_send,
@@ -130,24 +135,25 @@
 
     peers(greet)
     reps(greet_rep)
-    p_copy = pltpu.make_async_copy(p_hbm, p_v, p_sem)
+    p_copy = pltpu.make_async_copy(p_hbm, pt_v, p_sem)
     p_copy.start()
 
+    c_v[:, 0:64] = cand_ref[0]
+    c_v[:, 64:LANES] = cand_ref[1]
     omap = omap_ref[...]
     count = omap.shape[1]
-    wanted = to_col(cand_ref[...])
+    wanted = to_col(c_v[...])
     pos = pick(wanted == iota((LANES, count), 1), jnp.broadcast_to(omap, (LANES, count)))
     pos_row = to_row(pos)
     owner = pos_row >> 6
     row1 = (pos_row & 63) + 1
-    weights = w_ref[...]
+    x_s[:, 0, :] = jnp.where(owner == iota((G, LANES), 0), row1, 0).astype(F32)
+    y_r[me] = x_s[me]
+    q_all[pl.ds(2 * me, 2)] = q_ref[...]
+    t_r[me, 0:1, 0:64] = teach_ref[0]
+    t_r[me, 0:1, 64:LANES] = teach_ref[1]
     lane = iota((1, LANES), 1)
-    half = lane >> 6
-    mine_w = pick((lane & 63) == 0, weights)
-    x_s[:, 0, :] = jnp.where(owner == iota((G, LANES), 0), row1, 0).astype(F32)
-    x_s[:, 1, :] = jnp.broadcast_to(mine_w, (G, LANES))
-    q_all[pl.ds(2 * me, 2)] = q_ref[...]
-    y_r[me] = x_s[me]
+    t_r[me, 1:2, :] = jnp.where(lane < 64, w_ref[0, 0], w_ref[0, 1])
 
     pl.semaphore_wait(barrier, G - 1 + R - 1)
 
@@ -159,8 +165,12 @@
             q_ref, q_all.at[pl.ds(2 * me, 2)], q_send.at[g], q_recv.at[me], g, rep
         ).start()
 
+    def send_t(g):
+        remote(t_r.at[me], t_r.at[me], t_send.at[g], t_recv.at[me], g, rep).start()
+
     peers(send_y)
     peers(send_q)
+    peers(send_t)
 
     def wait_y(g):
         remote(x_s.at[g], y_r.at[g], y_send.at[g], y_recv.at[g], g, rep).wait_recv()
@@ -171,14 +181,6 @@
         ).wait_recv()
 
     peers(wait_y)
-
-    group_w = jnp.sum(y_r[:, 1, :], axis=0, keepdims=True)
-    wr[rep] = group_w
-
-    def send_w(r):
-        remote(wr.at[rep], wr.at[rep], w_send.at[r], w_recv.at[rep], me, r).start()
-
-    reps(send_w)
 
     y = y_r[:, 0, :].astype(I32)
     have = y > 0
@@ -224,8 +226,36 @@
     meta_copy.start()
     m_v[...] = jnp.zeros_like(m_v)
     meta_copy.wait()
+
     p_copy.wait()
+    pitch = p_f.shape[0] // stored
+
+    def spread(i, carry):
+        for u in range(4):
+            j = i * 4 + u
+            p_f[pl.ds(j, stored, stride=pitch), :] = pt_v[j].astype(F32)
+        return carry
+
+    lax.fori_loop(0, token_len // 4, spread, 0)
+
+    def settle(p, carry):
+        p_v[p] = p_f[pl.ds(pl.multiple_of(p * pitch, 8), token_len), :].astype(BF16)
+        return carry
+
+    lax.fori_loop(0, stored, settle, 0)
     peers(wait_q)
+
+    def wait_t(g):
+        remote(t_r.at[g], t_r.at[g], t_send.at[g], t_recv.at[g], g, rep).wait_recv()
+
+    peers(wait_t)
+
+    wr[rep] = jnp.sum(t_r[:, 1, :], axis=0, keepdims=True)
+
+    def send_w(r):
+        remote(wr.at[rep], wr.at[rep], w_send.at[r], w_recv.at[rep], me, r).start()
+
+    reps(send_w)
 
     def query_of(b, ch):
         return q_all[(meta_s[b, ch] >> 6) & (2 * G - 1)]
@@ -263,14 +293,24 @@
         row = to_row(pick(block == b, matched))
         hit = loc_cols == iota((nslot, LANES), 1) * WIDE + b
         scores += pick(hit, jnp.broadcast_to(row, (nslot, LANES)))
-    score_rows = jnp.zeros((G, LANES), F32)
-    for k in range(CAP):
-        score_rows += jnp.where(slotr[k] == ylane, scores[k * G : (k + 1) * G, :], 0.0)
-    v_s[:, 0, :] = score_rows
-    v_r[me] = v_s[me]
+    slots = [slotr[k][:, 0:1] for k in range(CAP)]
+    score = [scores[k * G : (k + 1) * G, :] for k in range(CAP)]
+    belongs = [[(r >= 0) & (r < 64) for r in slots], [r >= 64 for r in slots]]
+    spot = ylane - iota((G, LANES), 0)
+    stats = jnp.zeros((1, LANES), F32)
+    for h in (0, 1):
+        top = jnp.full((G, 1), LOW, F32)
+        for k in range(CAP):
+            top = jnp.maximum(top, jnp.where(belongs[h][k], score[k], LOW))
+        total = jnp.zeros((G, 1), F32)
+        for k in range(CAP):
+            total += jnp.where(belongs[h][k], jnp.exp(score[k] - top), 0.0)
+        for col, shift in ((top, h * G), (total, 64 + h * G)):
+            stats += jnp.sum(jnp.where(spot == shift, col, 0.0), axis=0, keepdims=True)
+    v_r[me] = stats
 
     def send_v(g):
-        remote(v_s.at[g], v_r.at[me], v_send.at[g], v_recv.at[me], g, rep).start()
+        remote(v_r.at[me], v_r.at[me], v_send.at[g], v_recv.at[me], g, rep).start()
 
     peers(send_v)
 
@@ -287,57 +327,55 @@
 
     lax.fori_loop(0, NCH // UNROLL, lift_group, 0)
 
+    teacher = t_r[:, 0, :]
+    half = ylane >> 6
+    top = [jnp.max(jnp.where(half == h, teacher, LOW), axis=1, keepdims=True) for h in (0, 1)]
+    shifted = teacher - jnp.where(half == 0, top[0], top[1])
+    powers = jnp.exp(shifted)
+    total = [pick(half == h, powers) for h in (0, 1)]
+    log_teacher = shifted - jnp.log(jnp.where(half == 0, total[0], total[1]))
+    weight = [pick(ylane == h * 64, t_r[:, 1, :]) for h in (0, 1)]
+
     def wait_v(g):
-        remote(v_s.at[g], v_r.at[g], v_send.at[g], v_recv.at[g], g, rep).wait_recv()
+        remote(v_r.at[g], v_r.at[g], v_send.at[g], v_recv.at[g], g, rep).wait_recv()
 
     def wait_w(r):
         remote(wr.at[r], wr.at[r], w_send.at[r], w_recv.at[r], me, r).wait_recv()
 
+    reps(wait_w)
+    by_rep = jnp.sum(wr[...], axis=0)
+    weight_sum = jnp.sum(jnp.where((lane & 63) == 0, by_rep, 0.0), axis=1, keepdims=True)
     peers(wait_v)
-    reps(wait_w)
-
-    def log_softmax(values):
-        top = [jnp.max(jnp.where(half == h, values, -3e38), axis=1, keepdims=True) for h in (0, 1)]
-        shifted = values - jnp.where(half == 0, top[0], top[1])
-        e = jnp.exp(shifted)
-        total = [pick(half == h, e) for h in (0, 1)]
-        return shifted - jnp.log(jnp.where(half == 0, total[0], total[1]))
-
-    log_student = log_softmax(jnp.sum(v_r[...], axis=0))
-    log_teacher = log_softmax(teach_ref[...])
-    teacher_prob = jnp.exp(log_teacher)
-    weight_sum = jnp.sum(wr[...], axis=0)
+
+    stats = v_r[:, 0, :]
+    top = jnp.max(stats, axis=0, keepdims=True)
+    total = jnp.sum(pltpu.roll(stats, 64, 1) * jnp.exp(stats - top), axis=0, keepdims=True)
+    log_total = top + jnp.log(total)
+    log_totals = [pick(spot == h * G, jnp.broadcast_to(log_total, (G, LANES))) for h in (0, 1)]
+
     scale_all = 2.0 * G * R
-    score_grad = scale_all * weights / weight_sum * (jnp.exp(log_student) - teacher_prob)
-    part = jnp.sum(
-        weights * (teacher_prob * (log_teacher - log_student)), axis=1, keepdims=True
-    )
-    g_r[me] = jnp.concatenate([score_grad, jnp.broadcast_to(part, (1, LANES))], axis=0)
+    by_slot = []
+    part = jnp.zeros((G, 1), F32)
+    for k in range(CAP):
+        late = belongs[1][k]
+        valid = slots[k] >= 0
+        log_t = pick(slotr[k] == ylane, log_teacher)
+        log_s = score[k] - jnp.where(late, log_totals[1], log_totals[0])
+        w = jnp.where(late, weight[1], weight[0])
+        prob_t = jnp.exp(log_t)
+        grad = scale_all * w / weight_sum * (jnp.exp(log_s) - prob_t)
+        grad = jnp.where(valid, grad, 0.0)
+        part += jnp.where(valid, w * (prob_t * (log_t - log_s)), 0.0)
+        by_slot.append(grad)
+        sgq[:, k, :] = jnp.broadcast_to(jnp.where(late, 0.0, grad), (G, LANES))
+        sgq[:, CAP + k, :] = jnp.broadcast_to(jnp.where(late, grad, 0.0), (G, LANES))
+    g_r[me] = jnp.broadcast_to(jnp.sum(part, axis=0, keepdims=True), (1, LANES))
 
     def send_g(g):
         remote(g_r.at[me], g_r.at[me], g_send.at[g], g_recv.at[me], g, rep).start()
 
     def wait_g(g):
         remote(g_r.at[g], g_r.at[g], g_send.at[g], g_recv.at[g], g, rep).wait_recv()
-
-    peers(send_g)
-    peers(wait_g)
-
-    lr[rep] = jnp.sum(g_r[:, 1, :], axis=0, keepdims=True)
-
-    def send_l(r):
-        remote(lr.at[rep], lr.at[rep], l_send.at[r], l_recv.at[rep], me, r).start()
-
-    reps(send_l)
-
-    grads = g_r[:, 0, :]
-    by_slot = []
-    for k in range(CAP):
-        rk = slotr[k]
-        col = pick(rk == ylane, grads)
-        by_slot.append(col)
-        sgq[:, k, :] = jnp.where(rk < 64, col, 0.0)
-        sgq[:, CAP + k, :] = jnp.where(rk >= 64, col, 0.0)
 
     def query_sum(s):
         scales = sgq[s]
@@ -360,6 +398,7 @@
         return carry
 
     lax.fori_loop(1, G, send_qg, 0)
+    peers(send_g)
     one, two = query_sum(me)
     qg_r[me, 0] = one
     qg_r[me, 1] = two
@@ -398,14 +437,29 @@
 
     lax.fori_loop(0, NCH // UNROLL, back_group, 0)
 
+    peers(wait_g)
+    lr[rep] = jnp.sum(g_r[...], axis=0)
+
+    def send_l(r):
+        remote(lr.at[rep], lr.at[rep], l_send.at[r], l_recv.at[rep], me, r).start()
+
+    reps(send_l)
+
     def place(p, carry):
         mark = meta_s[6, p]
-        p_v[p] = att[jnp.maximum(mark - 1, 0)] * jnp.where(mark > 0, 1.0, 0.0).astype(BF16)
+        rows = att[jnp.maximum(mark - 1, 0)].astype(F32) * jnp.where(mark > 0, 1.0, 0.0)
+        p_f[pl.ds(p, token_len, stride=stored), :] = rows
         return carry
 
     lax.fori_loop(0, stored, place, 0)
-    out_copy = pltpu.make_async_copy(p_v, pgrad_hbm, out_sem)
-    out_copy.start()
+
+    def pack(i, carry):
+        for u in range(4):
+            j = i * 4 + u
+            pgrad_ref[j] = p_f[pl.ds(pl.multiple_of(j * stored, stored), stored), :].astype(BF16)
+        return carry
+
+    lax.fori_loop(0, token_len // 4, pack, 0)
 
     def wait_l(r):
         remote(lr.at[r], lr.at[r], l_send.at[r], l_recv.at[r], me, r).wait_recv()
@@ -425,8 +479,9 @@
 
     def drain(g):
         remote(x_s.at[g], y_r.at[g], y_send.at[g], y_recv.at[g], g, rep).wait_send()
+        remote(t_r.at[g], t_r.at[g], t_send.at[g], t_recv.at[g], g, rep).wait_send()
         remote(q_ref, q_all.at[pl.ds(2 * g, 2)], q_send.at[g], q_recv.at[g], g, rep).wait_send()
-        remote(v_s.at[g], v_r.at[g], v_send.at[g], v_recv.at[g], g, rep).wait_send()
+        remote(v_r.at[g], v_r.at[g], v_send.at[g], v_recv.at[g], g, rep).wait_send()
         remote(g_r.at[g], g_r.at[g], g_send.at[g], g_recv.at[g], g, rep).wait_send()
         remote(qg_s.at[g], qg_r.at[g], o_send.at[g], o_recv.at[g], g, rep).wait_send()
 
@@ -436,7 +491,6 @@
 
     peers(drain)
     reps(drain_rep)
-    out_copy.wait()
 
 
 def on_device(G, R, queries, passages, lengths, cand_ids, owner_map, teacher, weights):
@@ -444,6 +498,7 @@
     stored, _, token_len, _ = passages.shape
     chunks = (G * CAP + (WIDE - 1) * stored) // WIDE
     NCH = -(-chunks // UNROLL) * UNROLL
+    pitch = -(-token_len // 8) * 8
     vmem = pl.BlockSpec(memory_space=pltpu.VMEM)
     smem = pl.BlockSpec(memory_space=pltpu.SMEM)
     hbm = pl.BlockSpec(memory_space=pl.ANY)
@@ -454,18 +509,21 @@
         out_shape=(
             shape((1, LANES), F32),
             shape((query_local, query_len, dim), F32),
-            shape((stored, token_len, dim), BF16),
+            pltpu.VMEM((token_len, stored, dim), BF16),
         ),
-        in_specs=[vmem, vmem, vmem, hbm, smem, vmem, vmem],
-        out_specs=(vmem, vmem, hbm),
+        in_specs=[vmem, vmem, vmem, hbm, smem, vmem, smem],
+        out_specs=(vmem, vmem, vmem),
         scratch_shapes=[
+            pltpu.VMEM((token_len, stored, dim), BF16),
+            pltpu.VMEM((stored * pitch, dim), F32),
             pltpu.VMEM((stored, token_len, dim), BF16),
             pltpu.VMEM((query_local * G, query_len, dim), BF16),
-            pltpu.VMEM((G, 2, LANES), F32),
+            pltpu.VMEM((1, LANES), I32),
+            pltpu.VMEM((G, 1, LANES), F32),
+            pltpu.VMEM((G, 1, LANES), F32),
             pltpu.VMEM((G, 2, LANES), F32),
             pltpu.VMEM((G, 1, LANES), F32),
             pltpu.VMEM((G, 1, LANES), F32),
-            pltpu.VMEM((G, 2, LANES), F32),
             pltpu.VMEM((R, 1, LANES), F32),
             pltpu.VMEM((R, 1, LANES), F32),
             pltpu.VMEM((8, LANES), I32),
@@ -482,23 +540,22 @@
             pltpu.VMEM((token_len, dim), F32),
             dma,
             dma,
-            dma,
         ]
-        + [dma((G,))] * 10
+        + [dma((G,))] * 12
         + [dma((R,))] * 4,
         compiler_params=pltpu.CompilerParams(
             collective_id=0, has_side_effects=True, vmem_limit_bytes=56 * 1024 * 1024
         ),
     )(
-        cand_ids.reshape(1, LANES),
+        cand_ids,
         owner_map,
         queries.reshape(query_local, query_len, dim),
-        passages.reshape(stored, token_len, dim),
+        jnp.transpose(passages[:, 0], (1, 0, 2)),
         lengths.reshape(1, stored),
-        teacher.reshape(1, LANES),
-        jnp.repeat(weights.reshape(query_local), LANES // query_local).reshape(1, LANES),
+        teacher,
+        weights.reshape(1, query_local),
     )
-    return loss[0, 0], qgrad[:, None], pgrad[:, None]
+    return loss[0, 0], qgrad[:, None], jnp.transpose(pgrad, (1, 0, 2))[:, None]
 
 
 def solution(mesh):

time: 81.1 us -> 73 us (0.900)
  local copies, waits for them, and re-layouts: 13.7 us -> 2.23 us
  Pallas kernels: 62.3 us -> 68.2 us
  other arithmetic: 2.68 us -> 0 us
    unnamed x9 -> x6, local copies, waits for them, and re-layouts: 11.2 us -> 2.23 us
    pallas_call x1, Pallas kernels: 62.3 us -> 68.2 us  [on_device(): pl.pallas_call(functools.partial(step_kernel, G, R, NCH), out_shape=(shap...]
    unnamed x2 -> x0, other arithmetic: 2.68 us -> none
    reshape x2 -> x0, local copies, waits for them, and re-layouts: 1.19 us -> none  [the longest x1 0.59 us: on_device(): cand_ids.reshape(1, LANES)]
where the time goes in v2:
time: 73 us; the launch traced here: 72.3 us
  Pallas kernels  68.2 us (93%)
  local copies, waits for them, and re-layouts  2.23 us (3%)
  between operations  1.84 us (3%)
    pallas_call x1, Pallas kernels, on_device(): pl.pallas_call(functools.partial(step_kernel, G, R, NCH), out_shape=(shap...  68.2 us
    unnamed x6, local copies, waits for them, and re-layouts  2.23 us

profile of v2, /device:TPU:2, one launch (start us, length us, event | category | flops | bytes accessed | tf_op | source)
XLA Modules:
  0.0 72.3 jit_solution(1738714109509442326)
XLA Ops:
  0.6 68.2 %shard_map.94 = (f32[1,128]{1,0:T(1,128)}, f32[2,32,128]{2,1,0:T(8,128)}, bf16[180,64,128]{2,1,0:T(8,128)(2,1)S(1)}) custom-call(s32[2,1,64]{2,1,0:T(1,128)} %cand_ref.1, s32[1,2048]{1,0:T(1,128)} %omap_ref.1, bf16[2,32,128]{2,1,0:T(8,128)(2,1)} %bitcast.17, bf16[180,64,128]{2,1,0:T(8,128)(2,1)} %bitcast.15, s32[1,64]{1,0:T(1,128)} %bitcast.18, ...), custom_call_target="tpu_custom_call" | custom-call | tf_op jit(solution)/shard_map/pallas_call | solution.py:507
  68.9 0.0 copy-start.1
  68.9 0.0 copy-start
  68.9 1.6 %copy.14 = bf16[64,1,180,128]{3,0,2,1:T(8,128)(2,1)} copy(bf16[64,1,180,128]{3,0,2,1:T(8,128)(2,1)S(1)} %bitcast.14) | data formatting | bytes 5898240
  70.5 0.0 copy-done.1
  70.5 0.0 copy-done
  70.5 0.6 copy.16
Async XLA Ops:
  68.9 1.6 %copy-start.1 = (f32[1,128]{1,0:T(1,128)S(1)}, f32[1,128]{1,0:T(1,128)}, u32[]{:S(2)}) copy-start(f32[1,128]{1,0:T(1,128)} %get-tuple-element.6) | copy-start | bytes 1540
  68.9 1.7 %copy-start = (f32[2,32,128]{2,1,0:T(8,128)S(1)}, f32[2,32,128]{2,1,0:T(8,128)}, u32[]{:S(2)}) copy-start(f32[2,32,128]{2,1,0:T(8,128)} %get-tuple-element.7) | copy-start | bytes 98308

commit v3 on v2

--- a/solution.py
+++ b/solution.py
@@ -19,6 +19,7 @@
 WIDE = 4
 UNROLL = 8
 LOW = -3e38
+YN = 4
 
 
 def iota(shape, axis):
@@ -60,11 +61,11 @@
     p_v,
     q_all,
     c_v,
-    x_s,
-    y_r,
     t_r,
-    v_r,
-    g_r,
+    vz,
+    vy,
+    gz_r,
+    gy_r,
     wr,
     lr,
     meta_v,
@@ -76,23 +77,34 @@
     loccol,
     sgq,
     sgl,
-    qg_s,
-    qg_r,
+    oy_s,
+    oy_r,
+    oz_s,
+    oz_r,
+    own,
     acc,
     p_sem,
     meta_sem,
-    y_send,
-    y_recv,
-    q_send,
-    q_recv,
-    t_send,
-    t_recv,
-    v_send,
-    v_recv,
-    g_send,
-    g_recv,
-    o_send,
-    o_recv,
+    ty_send,
+    ty_recv,
+    qy_send,
+    qy_recv,
+    oy_send,
+    oy_recv,
+    tz_send,
+    tz_recv,
+    qz_send,
+    qz_recv,
+    oz_send,
+    oz_recv,
+    vz_send,
+    vz_recv,
+    gz_send,
+    gz_recv,
+    vy_send,
+    vy_recv,
+    gy_send,
+    gy_recv,
     w_send,
     w_recv,
     l_send,
@@ -100,6 +112,8 @@
 ):
     me = lax.axis_index("grp")
     rep = lax.axis_index("rep")
+    ZN = G // YN
+    z, y = me // YN, lax.rem(me, YN)
     stored, token_len, dim = p_v.shape
     query_len = q_ref.shape[1]
     nslot = G * CAP
@@ -114,27 +128,33 @@
             device_id_type=MESH,
         )
 
-    def peers(body):
+    def near_z(t):
+        odd = lax.rem(t, 2)
+        return lax.rem(z + odd * ((t + 1) // 2) + (1 - odd) * (ZN - t // 2), ZN)
+
+    def over_z(body, far=False):
         def one(t, carry):
-            body(lax.rem(me + t, G))
+            body(near_z(ZN - t if far else t))
             return carry
 
-        lax.fori_loop(1, G, one, 0)
-
-    def reps(body):
+        lax.fori_loop(1, ZN, one, 0)
+
+    def over_y(body):
+        for t in range(1, YN):
+            body(lax.rem(y + t, YN))
+
+    def over_rep(body):
         for t in range(1, R):
             body(lax.rem(rep + t, R))
 
     barrier = pltpu.get_barrier_semaphore()
 
-    def greet(g):
-        pl.semaphore_signal(barrier, inc=1, device_id=(g, rep), device_id_type=MESH)
-
-    def greet_rep(r):
-        pl.semaphore_signal(barrier, inc=1, device_id=(me, r), device_id_type=MESH)
-
-    peers(greet)
-    reps(greet_rep)
+    def greet(g, r):
+        pl.semaphore_signal(barrier, inc=1, device_id=(g, r), device_id_type=MESH)
+
+    over_z(lambda zz: greet(zz * YN + y, rep))
+    over_y(lambda yy: greet(z * YN + yy, rep))
+    over_rep(lambda rr: greet(me, rr))
     p_copy = pltpu.make_async_copy(p_hbm, pt_v, p_sem)
     p_copy.start()
 
@@ -144,50 +164,87 @@
     count = omap.shape[1]
     wanted = to_col(c_v[...])
     pos = pick(wanted == iota((LANES, count), 1), jnp.broadcast_to(omap, (LANES, count)))
-    pos_row = to_row(pos)
-    owner = pos_row >> 6
-    row1 = (pos_row & 63) + 1
-    x_s[:, 0, :] = jnp.where(owner == iota((G, LANES), 0), row1, 0).astype(F32)
-    y_r[me] = x_s[me]
-    q_all[pl.ds(2 * me, 2)] = q_ref[...]
+    lane = iota((1, LANES), 1)
     t_r[me, 0:1, 0:64] = teach_ref[0]
     t_r[me, 0:1, 64:LANES] = teach_ref[1]
-    lane = iota((1, LANES), 1)
     t_r[me, 1:2, :] = jnp.where(lane < 64, w_ref[0, 0], w_ref[0, 1])
-
-    pl.semaphore_wait(barrier, G - 1 + R - 1)
-
-    def send_y(g):
-        remote(x_s.at[g], y_r.at[me], y_send.at[g], y_recv.at[me], g, rep).start()
-
-    def send_q(g):
-        remote(
-            q_ref, q_all.at[pl.ds(2 * me, 2)], q_send.at[g], q_recv.at[me], g, rep
-        ).start()
-
-    def send_t(g):
-        remote(t_r.at[me], t_r.at[me], t_send.at[g], t_recv.at[me], g, rep).start()
-
-    peers(send_y)
-    peers(send_q)
-    peers(send_t)
-
-    def wait_y(g):
-        remote(x_s.at[g], y_r.at[g], y_send.at[g], y_recv.at[g], g, rep).wait_recv()
-
-    def wait_q(g):
-        remote(
-            q_ref, q_all.at[pl.ds(2 * g, 2)], q_send.at[g], q_recv.at[g], g, rep
-        ).wait_recv()
-
-    peers(wait_y)
-
-    y = y_r[:, 0, :].astype(I32)
-    have = y > 0
+    t_r[me, 2:3, :] = to_row(pos).astype(F32)
+    q_all[pl.ds(2 * me, 2)] = q_ref[...]
+
+    pl.semaphore_wait(barrier, ZN - 1 + YN - 1 + R - 1)
+
+    def t_z(to, src):
+        g = src * YN + y
+        return remote(t_r.at[g], t_r.at[g], tz_send.at[to], tz_recv.at[src], to * YN + y, rep)
+
+    def q_z(to, src):
+        rows = q_all.at[pl.ds(2 * (src * YN + y), 2)]
+        return remote(rows, rows, qz_send.at[to], qz_recv.at[src], to * YN + y, rep)
+
+    def t_y(to, g):
+        ssem = ty_send.at[g // YN * YN + to]
+        return remote(t_r.at[g], t_r.at[g], ssem, ty_recv.at[g], z * YN + to, rep)
+
+    def q_y(to, g):
+        rows = q_all.at[pl.ds(2 * g, 2)]
+        ssem = qy_send.at[g // YN * YN + to]
+        return remote(rows, rows, ssem, qy_recv.at[g], z * YN + to, rep)
+
+    over_z(lambda zz: t_z(zz, z).start())
+    over_y(lambda yy: t_y(yy, me).start())
+    over_z(lambda zz: q_z(zz, z).start())
+    over_y(lambda yy: q_y(yy, me).start())
+
+    def pass_t(zz):
+        t_z(z, zz).wait_recv()
+        over_y(lambda yy: t_y(yy, zz * YN + y).start())
+
+    def pass_q(zz):
+        q_z(z, zz).wait_recv()
+        over_y(lambda yy: q_y(yy, zz * YN + y).start())
+
+    over_z(pass_t)
+    over_z(pass_q)
+
+    p_copy.wait()
+    pitch = p_f.shape[0] // stored
+
+    def spread(i, carry):
+        for u in range(4):
+            j = i * 4 + u
+            p_f[pl.ds(j, stored, stride=pitch), :] = pt_v[j].astype(F32)
+        return carry
+
+    lax.fori_loop(0, token_len // 4, spread, 0)
+
+    def settle(p, carry):
+        p_v[p] = p_f[pl.ds(pl.multiple_of(p * pitch, 8), token_len), :].astype(BF16)
+        return carry
+
+    lax.fori_loop(0, stored, settle, 0)
+
+    def all_z(body):
+        def one(zz, carry):
+            body(zz)
+            return carry
+
+        lax.fori_loop(0, ZN, one, 0)
+
+    all_z(lambda zz: over_y(lambda yy: t_y(y, zz * YN + yy).wait_recv()))
+
+    wr[rep] = jnp.sum(t_r[:, 1, :], axis=0, keepdims=True)
+
+    def w_rep(to, src):
+        return remote(wr.at[src], wr.at[src], w_send.at[to], w_recv.at[src], me, to)
+
+    over_rep(lambda rr: w_rep(rr, rep).start())
+
+    spots = t_r[:, 2, :].astype(I32)
+    have = (spots >> 6) == me
     lower = (iota((LANES, LANES), 0) < iota((LANES, LANES), 1)).astype(BF16)
     before = jnp.dot(have.astype(F32).astype(BF16), lower, preferred_element_type=F32).astype(I32)
     ylane = iota((G, LANES), 1)
-    code = jnp.where(have, (y << 7) | ylane, 0)
+    code = jnp.where(have, (((spots & 63) + 1) << 7) | ylane, 0)
     codes = [pick(have & (before == k), code) for k in range(CAP)]
     for k in range(CAP):
         rk = jnp.where(codes[k] > 0, codes[k] & 127, -1)
@@ -227,35 +284,7 @@
     m_v[...] = jnp.zeros_like(m_v)
     meta_copy.wait()
 
-    p_copy.wait()
-    pitch = p_f.shape[0] // stored
-
-    def spread(i, carry):
-        for u in range(4):
-            j = i * 4 + u
-            p_f[pl.ds(j, stored, stride=pitch), :] = pt_v[j].astype(F32)
-        return carry
-
-    lax.fori_loop(0, token_len // 4, spread, 0)
-
-    def settle(p, carry):
-        p_v[p] = p_f[pl.ds(pl.multiple_of(p * pitch, 8), token_len), :].astype(BF16)
-        return carry
-
-    lax.fori_loop(0, stored, settle, 0)
-    peers(wait_q)
-
-    def wait_t(g):
-        remote(t_r.at[g], t_r.at[g], t_send.at[g], t_recv.at[g], g, rep).wait_recv()
-
-    peers(wait_t)
-
-    wr[rep] = jnp.sum(t_r[:, 1, :], axis=0, keepdims=True)
-
-    def send_w(r):
-        remote(wr.at[rep], wr.at[rep], w_send.at[r], w_recv.at[rep], me, r).start()
-
-    reps(send_w)
+    all_z(lambda zz: over_y(lambda yy: q_y(y, zz * YN + yy).wait_recv()))
 
     def query_of(b, ch):
         return q_all[(meta_s[b, ch] >> 6) & (2 * G - 1)]
@@ -307,12 +336,15 @@
             total += jnp.where(belongs[h][k], jnp.exp(score[k] - top), 0.0)
         for col, shift in ((top, h * G), (total, 64 + h * G)):
             stats += jnp.sum(jnp.where(spot == shift, col, 0.0), axis=0, keepdims=True)
-    v_r[me] = stats
-
-    def send_v(g):
-        remote(v_r.at[me], v_r.at[me], v_send.at[g], v_recv.at[me], g, rep).start()
-
-    peers(send_v)
+    vz[z] = stats
+
+    def v_z(to, src):
+        return remote(vz.at[src], vz.at[src], vz_send.at[to], vz_recv.at[src], to * YN + y, rep)
+
+    def v_y(to, src):
+        return remote(vy.at[src], vy.at[src], vy_send.at[to], vy_recv.at[src], z * YN + to, rep)
+
+    over_z(lambda zz: v_z(zz, z).start())
 
     def lift(ch):
         u = lax.dot_general(
@@ -325,7 +357,19 @@
             lift(g * UNROLL + u)
         return carry
 
-    lax.fori_loop(0, NCH // UNROLL, lift_group, 0)
+    groups = NCH // UNROLL
+    lax.fori_loop(0, groups // 2, lift_group, 0)
+
+    def combine(stats):
+        top = jnp.max(stats, axis=0, keepdims=True)
+        total = jnp.sum(pltpu.roll(stats, 64, 1) * jnp.exp(stats - top), axis=0, keepdims=True)
+        return top, total
+
+    over_z(lambda zz: v_z(z, zz).wait_recv())
+    top, total = combine(vz[:, 0, :])
+    vy[y] = jnp.where(lane < 64, top, pltpu.roll(total, 64, 1))
+    over_y(lambda yy: v_y(yy, y).start())
+    lax.fori_loop(groups // 2, groups, lift_group, 0)
 
     teacher = t_r[:, 0, :]
     half = ylane >> 6
@@ -336,20 +380,11 @@
     log_teacher = shifted - jnp.log(jnp.where(half == 0, total[0], total[1]))
     weight = [pick(ylane == h * 64, t_r[:, 1, :]) for h in (0, 1)]
 
-    def wait_v(g):
-        remote(v_r.at[g], v_r.at[g], v_send.at[g], v_recv.at[g], g, rep).wait_recv()
-
-    def wait_w(r):
-        remote(wr.at[r], wr.at[r], w_send.at[r], w_recv.at[r], me, r).wait_recv()
-
-    reps(wait_w)
+    over_rep(lambda rr: w_rep(rep, rr).wait_recv())
     by_rep = jnp.sum(wr[...], axis=0)
     weight_sum = jnp.sum(jnp.where((lane & 63) == 0, by_rep, 0.0), axis=1, keepdims=True)
-    peers(wait_v)
-
-    stats = v_r[:, 0, :]
-    top = jnp.max(stats, axis=0, keepdims=True)
-    total = jnp.sum(pltpu.roll(stats, 64, 1) * jnp.exp(stats - top), axis=0, keepdims=True)
+    over_y(lambda yy: v_y(y, yy).wait_recv())
+    top, total = combine(vy[:, 0, :])
     log_total = top + jnp.log(total)
     log_totals = [pick(spot == h * G, jnp.broadcast_to(log_total, (G, LANES))) for h in (0, 1)]
 
@@ -369,13 +404,18 @@
         by_slot.append(grad)
         sgq[:, k, :] = jnp.broadcast_to(jnp.where(late, 0.0, grad), (G, LANES))
         sgq[:, CAP + k, :] = jnp.broadcast_to(jnp.where(late, grad, 0.0), (G, LANES))
-    g_r[me] = jnp.broadcast_to(jnp.sum(part, axis=0, keepdims=True), (1, LANES))
-
-    def send_g(g):
-        remote(g_r.at[me], g_r.at[me], g_send.at[g], g_recv.at[me], g, rep).start()
-
-    def wait_g(g):
-        remote(g_r.at[g], g_r.at[g], g_send.at[g], g_recv.at[g], g, rep).wait_recv()
+    gz_r[z] = jnp.broadcast_to(jnp.sum(part, axis=0, keepdims=True), (1, LANES))
+
+    def g_z(to, src):
+        return remote(gz_r.at[src], gz_r.at[src], gz_send.at[to], gz_recv.at[src], to * YN + y, rep)
+
+    def g_y(to, src):
+        return remote(gy_r.at[src], gy_r.at[src], gy_send.at[to], gy_recv.at[src], z * YN + to, rep)
+
+    def l_rep(to, src):
+        return remote(lr.at[src], lr.at[src], l_send.at[to], l_recv.at[src], me, to)
+
+    over_z(lambda zz: g_z(zz, z).start())
 
     def query_sum(s):
         scales = sgq[s]
@@ -387,21 +427,34 @@
             u = u_v[at].astype(F32)
             one += scales[k : k + 1, :] * u
             two += scales[CAP + k : CAP + k + 1, :] * u
-        return one.astype(BF16), two.astype(BF16)
-
-    def send_qg(t, carry):
-        s = lax.rem(me + t, G)
-        one, two = query_sum(s)
-        qg_s[s, 0] = one
-        qg_s[s, 1] = two
-        remote(qg_s.at[s], qg_r.at[me], o_send.at[s], o_recv.at[me], s, rep).start()
-        return carry
-
-    lax.fori_loop(1, G, send_qg, 0)
-    peers(send_g)
-    one, two = query_sum(me)
-    qg_r[me, 0] = one
-    qg_r[me, 1] = two
+        return one, two
+
+    def o_y(to, zz, src):
+        ssem, rsem = oy_send.at[zz * YN + to], oy_recv.at[zz * YN + src]
+        dst = oy_r.at[zz * YN + src]
+        return remote(oy_s.at[zz * YN + to], dst, ssem, rsem, z * YN + to, rep)
+
+    def o_z(to, src):
+        return remote(oz_s.at[to], oz_r.at[src], oz_send.at[to], oz_recv.at[src], to * YN + y, rep)
+
+    def send_sums(zz):
+        def one_way(yy):
+            one, two = query_sum(zz * YN + yy)
+            oy_s[zz * YN + yy, 0] = one.astype(BF16)
+            oy_s[zz * YN + yy, 1] = two.astype(BF16)
+            o_y(yy, zz, y).start()
+
+        over_y(one_way)
+
+    over_z(send_sums, far=True)
+    send_sums(z)
+
+    def keep_sums(zz):
+        one, two = query_sum(zz * YN + y)
+        own[zz, 0] = one
+        own[zz, 1] = two
+
+    all_z(keep_sums)
 
     sg_row = to_row(jnp.concatenate(by_slot, axis=0))
     loc_rows = jnp.concatenate(
@@ -430,20 +483,36 @@
         att[ch] = total.astype(BF16)
 
     def back_group(i, carry):
-        g = NCH // UNROLL - 1 - i
+        g = groups - 1 - i
         for u in range(UNROLL):
             back(g * UNROLL + UNROLL - 1 - u)
         return carry
 
-    lax.fori_loop(0, NCH // UNROLL, back_group, 0)
-
-    peers(wait_g)
-    lr[rep] = jnp.sum(g_r[...], axis=0)
-
-    def send_l(r):
-        remote(lr.at[rep], lr.at[rep], l_send.at[r], l_recv.at[rep], me, r).start()
-
-    reps(send_l)
+    lax.fori_loop(0, groups, back_group, 0)
+
+    over_z(lambda zz: g_z(z, zz).wait_recv())
+    gy_r[y] = jnp.sum(gz_r[...], axis=0)
+    over_y(lambda yy: g_y(yy, y).start())
+
+    def line_sum(zz):
+        total = own[zz]
+
+        for t in range(1, YN):
+            yy = lax.rem(y + t, YN)
+            o_y(y, zz, yy).wait_recv()
+            total += oy_r[zz * YN + yy].astype(F32)
+        return total
+
+    def send_line(zz):
+        oz_s[zz] = line_sum(zz).astype(BF16)
+        o_z(zz, z).start()
+
+    over_z(send_line, far=True)
+    own[z] = line_sum(z)
+
+    over_y(lambda yy: g_y(y, yy).wait_recv())
+    lr[rep] = jnp.sum(gy_r[...], axis=0)
+    over_rep(lambda rr: l_rep(rr, rep).start())
 
     def place(p, carry):
         mark = meta_s[6, p]
@@ -461,36 +530,32 @@
 
     lax.fori_loop(0, token_len // 4, pack, 0)
 
-    def wait_l(r):
-        remote(lr.at[r], lr.at[r], l_send.at[r], l_recv.at[r], me, r).wait_recv()
-
-    reps(wait_l)
+    over_rep(lambda rr: l_rep(rep, rr).wait_recv())
     loss_ref[...] = jnp.sum(lr[...], axis=0) / weight_sum
 
-    def wait_o(g):
-        remote(qg_s.at[g], qg_r.at[g], o_send.at[g], o_recv.at[g], g, rep).wait_recv()
-
-    peers(wait_o)
-
-    def add(o, carry):
-        return carry + qg_r[o].astype(F32)
-
-    qgrad_ref[...] = lax.fori_loop(0, G, add, jnp.zeros(qgrad_ref.shape, F32))
-
-    def drain(g):
-        remote(x_s.at[g], y_r.at[g], y_send.at[g], y_recv.at[g], g, rep).wait_send()
-        remote(t_r.at[g], t_r.at[g], t_send.at[g], t_recv.at[g], g, rep).wait_send()
-        remote(q_ref, q_all.at[pl.ds(2 * g, 2)], q_send.at[g], q_recv.at[g], g, rep).wait_send()
-        remote(v_r.at[g], v_r.at[g], v_send.at[g], v_recv.at[g], g, rep).wait_send()
-        remote(g_r.at[g], g_r.at[g], g_send.at[g], g_recv.at[g], g, rep).wait_send()
-        remote(qg_s.at[g], qg_r.at[g], o_send.at[g], o_recv.at[g], g, rep).wait_send()
-
-    def drain_rep(r):
-        remote(wr.at[r], wr.at[r], w_send.at[r], w_recv.at[r], me, r).wait_send()
-        remote(lr.at[r], lr.at[r], l_send.at[r], l_recv.at[r], me, r).wait_send()
-
-    peers(drain)
-    reps(drain_rep)
+    qgrad_ref[...] = own[z]
+
+    def add(zz):
+        o_z(z, zz).wait_recv()
+        qgrad_ref[...] += oz_r[zz].astype(F32)
+
+    over_z(add)
+
+    def drain_z(zz):
+        for copy in (t_z, q_z, v_z, g_z, o_z):
+            copy(zz, z).wait_send()
+
+    def drain_y(zz, yy):
+        t_y(yy, zz * YN + y).wait_send()
+        q_y(yy, zz * YN + y).wait_send()
+        o_y(yy, zz, y).wait_send()
+
+    over_z(drain_z)
+    all_z(lambda zz: over_y(lambda yy: drain_y(zz, yy)))
+    over_y(lambda yy: v_y(yy, y).wait_send())
+    over_y(lambda yy: g_y(yy, y).wait_send())
+    over_rep(lambda rr: w_rep(rr, rep).wait_send())
+    over_rep(lambda rr: l_rep(rr, rep).wait_send())
 
 
 def on_device(G, R, queries, passages, lengths, cand_ids, owner_map, teacher, weights):
@@ -499,6 +564,7 @@
     chunks = (G * CAP + (WIDE - 1) * stored) // WIDE
     NCH = -(-chunks // UNROLL) * UNROLL
     pitch = -(-token_len // 8) * 8
+    ZN = G // YN
     vmem = pl.BlockSpec(memory_space=pltpu.VMEM)
     smem = pl.BlockSpec(memory_space=pltpu.SMEM)
     hbm = pl.BlockSpec(memory_space=pl.ANY)
@@ -519,11 +585,11 @@
             pltpu.VMEM((stored, token_len, dim), BF16),
             pltpu.VMEM((query_local * G, query_len, dim), BF16),
             pltpu.VMEM((1, LANES), I32),
-            pltpu.VMEM((G, 1, LANES), F32),
-            pltpu.VMEM((G, 1, LANES), F32),
-            pltpu.VMEM((G, 2, LANES), F32),
-            pltpu.VMEM((G, 1, LANES), F32),
-            pltpu.VMEM((G, 1, LANES), F32),
+            pltpu.VMEM((G, 3, LANES), F32),
+            pltpu.VMEM((ZN, 1, LANES), F32),
+            pltpu.VMEM((YN, 1, LANES), F32),
+            pltpu.VMEM((ZN, 1, LANES), F32),
+            pltpu.VMEM((YN, 1, LANES), F32),
             pltpu.VMEM((R, 1, LANES), F32),
             pltpu.VMEM((R, 1, LANES), F32),
             pltpu.VMEM((8, LANES), I32),
@@ -537,11 +603,16 @@
             pltpu.VMEM((LANES, WIDE, LANES), F32),
             pltpu.VMEM((G, query_local, query_len, dim), BF16),
             pltpu.VMEM((G, query_local, query_len, dim), BF16),
+            pltpu.VMEM((ZN, query_local, query_len, dim), BF16),
+            pltpu.VMEM((ZN, query_local, query_len, dim), BF16),
+            pltpu.VMEM((ZN, query_local, query_len, dim), F32),
             pltpu.VMEM((token_len, dim), F32),
             dma,
             dma,
         ]
-        + [dma((G,))] * 12
+        + [dma((G,))] * 6
+        + [dma((ZN,))] * 10
+        + [dma((YN,))] * 4
         + [dma((R,))] * 4,
         compiler_params=pltpu.CompilerParams(
             collective_id=0, has_side_effects=True, vmem_limit_bytes=56 * 1024 * 1024

time: 73 us -> 61.8 us (0.85)
  Pallas kernels: 68.2 us -> 57.6 us
    pallas_call x1, Pallas kernels: 68.2 us -> 57.6 us  [on_device(): pl.pallas_call(functools.partial(step_kernel, G, R, NCH), out_shape=(shap...]
where the time goes in v3:
time: 61.8 us; the launch traced here: 61.7 us
  Pallas kernels  57.6 us (93%)
  local copies, waits for them, and re-layouts  2.23 us (4%)
  between operations  1.84 us (3%)
    pallas_call x1, Pallas kernels, on_device(): pl.pallas_call(functools.partial(step_kernel, G, R, NCH), out_shape=(shap...  57.6 us
    unnamed x6, local copies, waits for them, and re-layouts  2.23 us

profile of v3, /device:TPU:2, one launch (start us, length us, event | category | flops | bytes accessed | tf_op | source)
XLA Modules:
  0.0 61.7 jit_solution(13657434901948232312)
XLA Ops:
  0.6 57.6 %shard_map.94 = (f32[1,128]{1,0:T(1,128)}, f32[2,32,128]{2,1,0:T(8,128)}, bf16[180,64,128]{2,1,0:T(8,128)(2,1)S(1)}) custom-call(s32[2,1,64]{2,1,0:T(1,128)} %cand_ref.1, s32[1,2048]{1,0:T(1,128)} %omap_ref.1, bf16[2,32,128]{2,1,0:T(8,128)(2,1)} %bitcast.17, bf16[180,64,128]{2,1,0:T(8,128)(2,1)} %bitcast.15, s32[1,64]{1,0:T(1,128)} %bitcast.18, ...), custom_call_target="tpu_custom_call" | custom-call | tf_op jit(solution)/shard_map/pallas_call | solution.py:573
  58.2 0.0 copy-start.1
  58.2 0.0 copy-start
  58.3 1.6 %copy.14 = bf16[64,1,180,128]{3,0,2,1:T(8,128)(2,1)} copy(bf16[64,1,180,128]{3,0,2,1:T(8,128)(2,1)S(1)} %bitcast.14) | data formatting | bytes 5898240
  59.9 0.0 copy-done.1
  59.9 0.0 copy-done
  59.9 0.6 %copy.16 = f32[2,1,32,128]{3,2,1,0:T(8,128)} copy(f32[2,1,32,128]{3,2,1,0:T(8,128)S(1)} %bitcast.16) | data formatting | bytes 65536
Async XLA Ops:
  58.2 1.6 %copy-start.1 = (f32[1,128]{1,0:T(1,128)S(1)}, f32[1,128]{1,0:T(1,128)}, u32[]{:S(2)}) copy-start(f32[1,128]{1,0:T(1,128)} %get-tuple-element.6) | copy-start | bytes 1540
  58.2 1.7 %copy-start = (f32[2,32,128]{2,1,0:T(8,128)S(1)}, f32[2,32,128]{2,1,0:T(8,128)}, u32[]{:S(2)}) copy-start(f32[2,32,128]{2,1,0:T(8,128)} %get-tuple-element.7) | copy-start | bytes 98308

commit v4 on v3

--- a/solution.py
+++ b/solution.py
@@ -62,8 +62,7 @@
     q_all,
     c_v,
     t_r,
-    vz,
-    vy,
+    v_r,
     gz_r,
     gy_r,
     wr,
@@ -91,18 +90,16 @@
     qy_recv,
     oy_send,
     oy_recv,
+    v_send,
+    v_recv,
     tz_send,
     tz_recv,
     qz_send,
     qz_recv,
     oz_send,
     oz_recv,
-    vz_send,
-    vz_recv,
     gz_send,
     gz_recv,
-    vy_send,
-    vy_recv,
     gy_send,
     gy_recv,
     w_send,
@@ -203,8 +200,15 @@
         q_z(z, zz).wait_recv()
         over_y(lambda yy: q_y(yy, zz * YN + y).start())
 
-    over_z(pass_t)
-    over_z(pass_q)
+    pass_t(near_z(1))
+
+    def pass_on(t, carry):
+        pass_t(near_z(t + 1))
+        pass_q(near_z(t))
+        return carry
+
+    lax.fori_loop(1, ZN - 1, pass_on, 0)
+    pass_q(near_z(ZN - 1))
 
     p_copy.wait()
     pitch = p_f.shape[0] // stored
@@ -336,15 +340,16 @@
             total += jnp.where(belongs[h][k], jnp.exp(score[k] - top), 0.0)
         for col, shift in ((top, h * G), (total, 64 + h * G)):
             stats += jnp.sum(jnp.where(spot == shift, col, 0.0), axis=0, keepdims=True)
-    vz[z] = stats
-
-    def v_z(to, src):
-        return remote(vz.at[src], vz.at[src], vz_send.at[to], vz_recv.at[src], to * YN + y, rep)
-
-    def v_y(to, src):
-        return remote(vy.at[src], vy.at[src], vy_send.at[to], vy_recv.at[src], z * YN + to, rep)
-
-    over_z(lambda zz: v_z(zz, z).start())
+    v_r[me] = stats
+
+    def v_to(to, src):
+        return remote(v_r.at[src], v_r.at[src], v_send.at[to], v_recv.at[src], to, rep)
+
+    def over_all(body):
+        over_z(lambda zz: [body(zz * YN + lax.rem(y + t, YN)) for t in (2, 1, 3, 0)] and None, far=True)
+        over_y(lambda yy: body(z * YN + yy))
+
+    over_all(lambda g: v_to(g, me).start())
 
     def lift(ch):
         u = lax.dot_general(
@@ -358,18 +363,7 @@
         return carry
 
     groups = NCH // UNROLL
-    lax.fori_loop(0, groups // 2, lift_group, 0)
-
-    def combine(stats):
-        top = jnp.max(stats, axis=0, keepdims=True)
-        total = jnp.sum(pltpu.roll(stats, 64, 1) * jnp.exp(stats - top), axis=0, keepdims=True)
-        return top, total
-
-    over_z(lambda zz: v_z(z, zz).wait_recv())
-    top, total = combine(vz[:, 0, :])
-    vy[y] = jnp.where(lane < 64, top, pltpu.roll(total, 64, 1))
-    over_y(lambda yy: v_y(yy, y).start())
-    lax.fori_loop(groups // 2, groups, lift_group, 0)
+    lax.fori_loop(0, groups, lift_group, 0)
 
     teacher = t_r[:, 0, :]
     half = ylane >> 6
@@ -383,8 +377,10 @@
     over_rep(lambda rr: w_rep(rep, rr).wait_recv())
     by_rep = jnp.sum(wr[...], axis=0)
     weight_sum = jnp.sum(jnp.where((lane & 63) == 0, by_rep, 0.0), axis=1, keepdims=True)
-    over_y(lambda yy: v_y(y, yy).wait_recv())
-    top, total = combine(vy[:, 0, :])
+    over_all(lambda g: v_to(me, g).wait_recv())
+    stats = v_r[:, 0, :]
+    top = jnp.max(stats, axis=0, keepdims=True)
+    total = jnp.sum(pltpu.roll(stats, 64, 1) * jnp.exp(stats - top), axis=0, keepdims=True)
     log_total = top + jnp.log(total)
     log_totals = [pick(spot == h * G, jnp.broadcast_to(log_total, (G, LANES))) for h in (0, 1)]
 
@@ -488,11 +484,14 @@
             back(g * UNROLL + UNROLL - 1 - u)
         return carry
 
-    lax.fori_loop(0, groups, back_group, 0)
-
+    lax.fori_loop(0, groups // 2, back_group, 0)
     over_z(lambda zz: g_z(z, zz).wait_recv())
     gy_r[y] = jnp.sum(gz_r[...], axis=0)
     over_y(lambda yy: g_y(yy, y).start())
+    lax.fori_loop(groups // 2, groups, back_group, 0)
+    over_y(lambda yy: g_y(y, yy).wait_recv())
+    lr[rep] = jnp.sum(gy_r[...], axis=0)
+    over_rep(lambda rr: l_rep(rr, rep).start())
 
     def line_sum(zz):
         total = own[zz]
@@ -510,10 +509,6 @@
     over_z(send_line, far=True)
     own[z] = line_sum(z)
 
-    over_y(lambda yy: g_y(y, yy).wait_recv())
-    lr[rep] = jnp.sum(gy_r[...], axis=0)
-    over_rep(lambda rr: l_rep(rr, rep).start())
-
     def place(p, carry):
         mark = meta_s[6, p]
         rows = att[jnp.maximum(mark - 1, 0)].astype(F32) * jnp.where(mark > 0, 1.0, 0.0)
@@ -542,7 +537,7 @@
     over_z(add)
 
     def drain_z(zz):
-        for copy in (t_z, q_z, v_z, g_z, o_z):
+        for copy in (t_z, q_z, g_z, o_z):
             copy(zz, z).wait_send()
 
     def drain_y(zz, yy):
@@ -552,7 +547,7 @@
 
     over_z(drain_z)
     all_z(lambda zz: over_y(lambda yy: drain_y(zz, yy)))
-    over_y(lambda yy: v_y(yy, y).wait_send())
+    over_all(lambda g: v_to(g, me).wait_send())
     over_y(lambda yy: g_y(yy, y).wait_send())
     over_rep(lambda rr: w_rep(rr, rep).wait_send())
     over_rep(lambda rr: l_rep(rr, rep).wait_send())
@@ -569,12 +564,11 @@
     smem = pl.BlockSpec(memory_space=pltpu.SMEM)
     hbm = pl.BlockSpec(memory_space=pl.ANY)
     dma = pltpu.SemaphoreType.DMA
-    shape = jax.ShapeDtypeStruct
     loss, qgrad, pgrad = pl.pallas_call(
         functools.partial(step_kernel, G, R, NCH),
         out_shape=(
-            shape((1, LANES), F32),
-            shape((query_local, query_len, dim), F32),
+            pltpu.VMEM((1, LANES), F32),
+            pltpu.VMEM((query_local, query_len, dim), F32),
             pltpu.VMEM((token_len, stored, dim), BF16),
         ),
         in_specs=[vmem, vmem, vmem, hbm, smem, vmem, smem],
@@ -586,8 +580,7 @@
             pltpu.VMEM((query_local * G, query_len, dim), BF16),
             pltpu.VMEM((1, LANES), I32),
             pltpu.VMEM((G, 3, LANES), F32),
-            pltpu.VMEM((ZN, 1, LANES), F32),
-            pltpu.VMEM((YN, 1, LANES), F32),
+            pltpu.VMEM((G, 1, LANES), F32),
             pltpu.VMEM((ZN, 1, LANES), F32),
             pltpu.VMEM((YN, 1, LANES), F32),
             pltpu.VMEM((R, 1, LANES), F32),
@@ -610,9 +603,9 @@
             dma,
             dma,
         ]
-        + [dma((G,))] * 6
-        + [dma((ZN,))] * 10
-        + [dma((YN,))] * 4
+        + [dma((G,))] * 8
+        + [dma((ZN,))] * 8
+        + [dma((YN,))] * 2
         + [dma((R,))] * 4,
         compiler_params=pltpu.CompilerParams(
             collective_id=0, has_side_effects=True, vmem_limit_bytes=56 * 1024 * 1024

time: 61.8 us -> 57.6 us (0.932)
  Pallas kernels: 57.6 us -> 53.5 us
    pallas_call x1, Pallas kernels: 57.6 us -> 53.5 us  [on_device(): pl.pallas_call(functools.partial(step_kernel, G, R, NCH), out_shape=(pltp...]
    unnamed x6 -> x2, local copies, waits for them, and re-layouts: 2.23 us -> 2.22 us
where the time goes in v4:
time: 57.6 us; the launch traced here: 57.5 us
  Pallas kernels  53.5 us (93%)
  local copies, waits for them, and re-layouts  2.22 us (4%)
  between operations  1.81 us (3%)
    pallas_call x1, Pallas kernels, on_device(): pl.pallas_call(functools.partial(step_kernel, G, R, NCH), out_shape=(pltp...  53.5 us
    unnamed x2, local copies, waits for them, and re-layouts  2.22 us

profile of v4, /device:TPU:2, one launch (start us, length us, event | category | flops | bytes accessed | tf_op | source)
XLA Modules:
  0.0 57.5 jit_solution(2698050518047135253)
XLA Ops:
  0.6 53.5 %shard_map.94 = (f32[1,128]{1,0:T(1,128)S(1)}, f32[2,32,128]{2,1,0:T(8,128)S(1)}, bf16[180,64,128]{2,1,0:T(8,128)(2,1)S(1)}) custom-call(s32[2,1,64]{2,1,0:T(1,128)} %cand_ref.1, s32[1,2048]{1,0:T(1,128)} %omap_ref.1, bf16[2,32,128]{2,1,0:T(8,128)(2,1)} %bitcast.18, bf16[180,64,128]{2,1,0:T(8,128)(2,1)} %bitcast.17, s32[1,64]{1,0:T(1,128)} %bitcast.19, ...), custom_call_target="tpu_custom_call" | custom-call | tf_op jit(solution)/shard_map/pallas_call | solution.py:567
  54.1 0.6 %copy.14 = f32[2,1,32,128]{3,2,1,0:T(8,128)} copy(f32[2,1,32,128]{3,2,1,0:T(8,128)S(1)} %bitcast.15) | data formatting | bytes 65536
  54.7 1.6 %copy.15 = bf16[64,1,180,128]{3,0,2,1:T(8,128)(2,1)} copy(bf16[64,1,180,128]{3,0,2,1:T(8,128)(2,1)S(1)} %bitcast.14) | data formatting | bytes 5898240

commit v5 on v4

--- a/solution.py
+++ b/solution.py
@@ -18,6 +18,7 @@
 CAP = 8
 WIDE = 4
 UNROLL = 8
+PART = 9
 LOW = -3e38
 YN = 4
 
@@ -46,16 +47,22 @@
     G,
     R,
     NCH,
+    cand_hbm,
+    omap_hbm,
+    q_hbm,
+    p_hbm,
+    len_hbm,
+    teach_hbm,
+    w_hbm,
+    loss_ref,
+    qgrad_ref,
+    pgrad_ref,
     cand_ref,
     omap_ref,
     q_ref,
-    p_hbm,
     len_ref,
     teach_ref,
     w_ref,
-    loss_ref,
-    qgrad_ref,
-    pgrad_ref,
     pt_v,
     p_f,
     p_v,
@@ -81,31 +88,30 @@
     oz_s,
     oz_r,
     own,
+    sums,
     acc,
+    in_sem,
     p_sem,
     meta_sem,
-    ty_send,
+    t_sent,
+    q_sent,
+    v_sent,
+    g_sent,
+    oy_sent,
+    oz_sent,
+    w_sent,
+    l_sent,
     ty_recv,
-    qy_send,
     qy_recv,
-    oy_send,
+    v_recv,
+    gz_recv,
+    gy_recv,
+    oz_recv,
+    w_recv,
+    l_recv,
+    tz_recv,
+    qz_recv,
     oy_recv,
-    v_send,
-    v_recv,
-    tz_send,
-    tz_recv,
-    qz_send,
-    qz_recv,
-    oz_send,
-    oz_recv,
-    gz_send,
-    gz_recv,
-    gy_send,
-    gy_recv,
-    w_send,
-    w_recv,
-    l_send,
-    l_recv,
 ):
     me = lax.axis_index("grp")
     rep = lax.axis_index("rep")
@@ -125,6 +131,10 @@
             device_id_type=MESH,
         )
 
+    def finish(like, count, sem):
+        blocks = like.at[pl.ds(0, count)]
+        pltpu.make_async_copy(blocks, blocks, sem).wait()
+
     def near_z(t):
         odd = lax.rem(t, 2)
         return lax.rem(z + odd * ((t + 1) // 2) + (1 - odd) * (ZN - t // 2), ZN)
@@ -152,8 +162,25 @@
     over_z(lambda zz: greet(zz * YN + y, rep))
     over_y(lambda yy: greet(z * YN + yy, rep))
     over_rep(lambda rr: greet(me, rr))
+    inputs = [
+        pltpu.make_async_copy(src, dst, in_sem.at[i])
+        for i, (src, dst) in enumerate(
+            (
+                (cand_hbm, cand_ref),
+                (omap_hbm, omap_ref),
+                (q_hbm, q_ref),
+                (teach_hbm, teach_ref),
+                (w_hbm, w_ref),
+                (len_hbm, len_ref),
+            )
+        )
+    ]
+    for copy in inputs:
+        copy.start()
     p_copy = pltpu.make_async_copy(p_hbm, pt_v, p_sem)
     p_copy.start()
+    for copy in inputs:
+        copy.wait()
 
     c_v[:, 0:64] = cand_ref[0]
     c_v[:, 64:LANES] = cand_ref[1]
@@ -172,20 +199,18 @@
 
     def t_z(to, src):
         g = src * YN + y
-        return remote(t_r.at[g], t_r.at[g], tz_send.at[to], tz_recv.at[src], to * YN + y, rep)
+        return remote(t_r.at[g], t_r.at[g], t_sent, tz_recv.at[src], to * YN + y, rep)
 
     def q_z(to, src):
         rows = q_all.at[pl.ds(2 * (src * YN + y), 2)]
-        return remote(rows, rows, qz_send.at[to], qz_recv.at[src], to * YN + y, rep)
+        return remote(rows, rows, q_sent, qz_recv.at[src], to * YN + y, rep)
 
     def t_y(to, g):
-        ssem = ty_send.at[g // YN * YN + to]
-        return remote(t_r.at[g], t_r.at[g], ssem, ty_recv.at[g], z * YN + to, rep)
+        return remote(t_r.at[g], t_r.at[g], t_sent, ty_recv, z * YN + to, rep)
 
     def q_y(to, g):
         rows = q_all.at[pl.ds(2 * g, 2)]
-        ssem = qy_send.at[g // YN * YN + to]
-        return remote(rows, rows, ssem, qy_recv.at[g], z * YN + to, rep)
+        return remote(rows, rows, q_sent, qy_recv, z * YN + to, rep)
 
     over_z(lambda zz: t_z(zz, z).start())
     over_y(lambda yy: t_y(yy, me).start())
@@ -199,16 +224,6 @@
     def pass_q(zz):
         q_z(z, zz).wait_recv()
         over_y(lambda yy: q_y(yy, zz * YN + y).start())
-
-    pass_t(near_z(1))
-
-    def pass_on(t, carry):
-        pass_t(near_z(t + 1))
-        pass_q(near_z(t))
-        return carry
-
-    lax.fori_loop(1, ZN - 1, pass_on, 0)
-    pass_q(near_z(ZN - 1))
 
     p_copy.wait()
     pitch = p_f.shape[0] // stored
@@ -221,11 +236,23 @@
 
     lax.fori_loop(0, token_len // 4, spread, 0)
 
-    def settle(p, carry):
-        p_v[p] = p_f[pl.ds(pl.multiple_of(p * pitch, 8), token_len), :].astype(BF16)
+    def settle(t):
+        for u in range(stored // ZN):
+            p = t * (stored // ZN) + u
+            p_v[p] = p_f[pl.ds(pl.multiple_of(p * pitch, 8), token_len), :].astype(BF16)
+
+    pass_t(near_z(1))
+
+    def pass_on(t, carry):
+        pass_t(near_z(t + 1))
+        pass_q(near_z(t))
+        settle(t)
         return carry
 
-    lax.fori_loop(0, stored, settle, 0)
+    lax.fori_loop(1, ZN - 1, pass_on, 0)
+    pass_q(near_z(ZN - 1))
+    settle(0)
+    settle(ZN - 1)
 
     def all_z(body):
         def one(zz, carry):
@@ -234,12 +261,12 @@
 
         lax.fori_loop(0, ZN, one, 0)
 
-    all_z(lambda zz: over_y(lambda yy: t_y(y, zz * YN + yy).wait_recv()))
+    finish(t_r, ZN * (YN - 1), ty_recv)
 
     wr[rep] = jnp.sum(t_r[:, 1, :], axis=0, keepdims=True)
 
     def w_rep(to, src):
-        return remote(wr.at[src], wr.at[src], w_send.at[to], w_recv.at[src], me, to)
+        return remote(wr.at[src], wr.at[src], w_sent, w_recv, me, to)
 
     over_rep(lambda rr: w_rep(rr, rep).start())
 
@@ -288,7 +315,7 @@
     m_v[...] = jnp.zeros_like(m_v)
     meta_copy.wait()
 
-    all_z(lambda zz: over_y(lambda yy: q_y(y, zz * YN + yy).wait_recv()))
+    finish(q_all, 2 * ZN * (YN - 1), qy_recv)
 
     def query_of(b, ch):
         return q_all[(meta_s[b, ch] >> 6) & (2 * G - 1)]
@@ -343,7 +370,7 @@
     v_r[me] = stats
 
     def v_to(to, src):
-        return remote(v_r.at[src], v_r.at[src], v_send.at[to], v_recv.at[src], to, rep)
+        return remote(v_r.at[src], v_r.at[src], v_sent, v_recv, to, rep)
 
     def over_all(body):
         over_z(lambda zz: [body(zz * YN + lax.rem(y + t, YN)) for t in (2, 1, 3, 0)] and None, far=True)
@@ -374,10 +401,10 @@
     log_teacher = shifted - jnp.log(jnp.where(half == 0, total[0], total[1]))
     weight = [pick(ylane == h * 64, t_r[:, 1, :]) for h in (0, 1)]
 
-    over_rep(lambda rr: w_rep(rep, rr).wait_recv())
+    finish(wr, R - 1, w_recv)
     by_rep = jnp.sum(wr[...], axis=0)
     weight_sum = jnp.sum(jnp.where((lane & 63) == 0, by_rep, 0.0), axis=1, keepdims=True)
-    over_all(lambda g: v_to(me, g).wait_recv())
+    finish(v_r, G - 1, v_recv)
     stats = v_r[:, 0, :]
     top = jnp.max(stats, axis=0, keepdims=True)
     total = jnp.sum(pltpu.roll(stats, 64, 1) * jnp.exp(stats - top), axis=0, keepdims=True)
@@ -403,13 +430,13 @@
     gz_r[z] = jnp.broadcast_to(jnp.sum(part, axis=0, keepdims=True), (1, LANES))
 
     def g_z(to, src):
-        return remote(gz_r.at[src], gz_r.at[src], gz_send.at[to], gz_recv.at[src], to * YN + y, rep)
+        return remote(gz_r.at[src], gz_r.at[src], g_sent, gz_recv, to * YN + y, rep)
 
     def g_y(to, src):
-        return remote(gy_r.at[src], gy_r.at[src], gy_send.at[to], gy_recv.at[src], z * YN + to, rep)
+        return remote(gy_r.at[src], gy_r.at[src], g_sent, gy_recv, z * YN + to, rep)
 
     def l_rep(to, src):
-        return remote(lr.at[src], lr.at[src], l_send.at[to], l_recv.at[src], me, to)
+        return remote(lr.at[src], lr.at[src], l_sent, l_recv, me, to)
 
     over_z(lambda zz: g_z(zz, z).start())
 
@@ -426,12 +453,11 @@
         return one, two
 
     def o_y(to, zz, src):
-        ssem, rsem = oy_send.at[zz * YN + to], oy_recv.at[zz * YN + src]
         dst = oy_r.at[zz * YN + src]
-        return remote(oy_s.at[zz * YN + to], dst, ssem, rsem, z * YN + to, rep)
+        return remote(oy_s.at[zz * YN + to], dst, oy_sent, oy_recv.at[zz], z * YN + to, rep)
 
     def o_z(to, src):
-        return remote(oz_s.at[to], oz_r.at[src], oz_send.at[to], oz_recv.at[src], to * YN + y, rep)
+        return remote(oz_s.at[to], oz_r.at[src], oz_sent, oz_recv, to * YN + y, rep)
 
     def send_sums(zz):
         def one_way(yy):
@@ -463,7 +489,7 @@
 
     acc[...] = jnp.zeros_like(acc)
 
-    def back(ch):
+    def back(ch, total):
         scales = sgl[ch]
         scaled = jnp.concatenate(
             [
@@ -474,32 +500,29 @@
         )
         product = jnp.dot(att[ch], scaled, preferred_element_type=F32)
         follows = (meta_s[0, ch] >> 12) == (meta_s[0, ch + 1] >> 12)
-        total = product + acc[...] * jnp.where(follows, 1.0, 0.0)
-        acc[...] = total
-        att[ch] = total.astype(BF16)
+        total = product + total * jnp.where(follows, 1.0, 0.0)
+        sums[ch] = total.astype(BF16)
+        return total
 
     def back_group(i, carry):
         g = groups - 1 - i
+        total = acc[...]
         for u in range(UNROLL):
-            back(g * UNROLL + UNROLL - 1 - u)
+            total = back(g * UNROLL + UNROLL - 1 - u, total)
+        acc[...] = total
         return carry
 
-    lax.fori_loop(0, groups // 2, back_group, 0)
-    over_z(lambda zz: g_z(z, zz).wait_recv())
+    lax.fori_loop(0, min(PART, groups), back_group, 0)
+    finish(gz_r, ZN - 1, gz_recv)
     gy_r[y] = jnp.sum(gz_r[...], axis=0)
     over_y(lambda yy: g_y(yy, y).start())
-    lax.fori_loop(groups // 2, groups, back_group, 0)
-    over_y(lambda yy: g_y(y, yy).wait_recv())
-    lr[rep] = jnp.sum(gy_r[...], axis=0)
-    over_rep(lambda rr: l_rep(rr, rep).start())
+    lax.fori_loop(min(PART, groups), groups, back_group, 0)
 
     def line_sum(zz):
+        finish(oy_r, YN - 1, oy_recv.at[zz])
         total = own[zz]
-
         for t in range(1, YN):
-            yy = lax.rem(y + t, YN)
-            o_y(y, zz, yy).wait_recv()
-            total += oy_r[zz * YN + yy].astype(F32)
+            total += oy_r[zz * YN + lax.rem(y + t, YN)].astype(F32)
         return total
 
     def send_line(zz):
@@ -508,14 +531,19 @@
 
     over_z(send_line, far=True)
     own[z] = line_sum(z)
-
-    def place(p, carry):
-        mark = meta_s[6, p]
-        rows = att[jnp.maximum(mark - 1, 0)].astype(F32) * jnp.where(mark > 0, 1.0, 0.0)
-        p_f[pl.ds(p, token_len, stride=stored), :] = rows
+    finish(gy_r, YN - 1, gy_recv)
+    lr[rep] = jnp.sum(gy_r[...], axis=0)
+    over_rep(lambda rr: l_rep(rr, rep).start())
+
+    def place(i, carry):
+        for u in range(4):
+            p = i * 4 + u
+            mark = meta_s[6, p]
+            rows = sums[jnp.maximum(mark - 1, 0)].astype(F32) * jnp.where(mark > 0, 1.0, 0.0)
+            p_f[pl.ds(p, token_len, stride=stored), :] = rows
         return carry
 
-    lax.fori_loop(0, stored, place, 0)
+    lax.fori_loop(0, stored // 4, place, 0)
 
     def pack(i, carry):
         for u in range(4):
@@ -525,32 +553,23 @@
 
     lax.fori_loop(0, token_len // 4, pack, 0)
 
-    over_rep(lambda rr: l_rep(rep, rr).wait_recv())
+    finish(t_r, G - 1, t_sent)
+    finish(q_all, 2 * (G - 1), q_sent)
+    finish(v_r, G - 1, v_sent)
+    finish(v_r, ZN + YN - 2, g_sent)
+    finish(oy_s, ZN * (YN - 1), oy_sent)
+    finish(oz_s, ZN - 1, oz_sent)
+    finish(wr, R - 1, w_sent)
+    finish(lr, R - 1, l_sent)
+
+    finish(lr, R - 1, l_recv)
     loss_ref[...] = jnp.sum(lr[...], axis=0) / weight_sum
 
-    qgrad_ref[...] = own[z]
-
-    def add(zz):
-        o_z(z, zz).wait_recv()
-        qgrad_ref[...] += oz_r[zz].astype(F32)
-
-    over_z(add)
-
-    def drain_z(zz):
-        for copy in (t_z, q_z, g_z, o_z):
-            copy(zz, z).wait_send()
-
-    def drain_y(zz, yy):
-        t_y(yy, zz * YN + y).wait_send()
-        q_y(yy, zz * YN + y).wait_send()
-        o_y(yy, zz, y).wait_send()
-
-    over_z(drain_z)
-    all_z(lambda zz: over_y(lambda yy: drain_y(zz, yy)))
-    over_all(lambda g: v_to(g, me).wait_send())
-    over_y(lambda yy: g_y(yy, y).wait_send())
-    over_rep(lambda rr: w_rep(rr, rep).wait_send())
-    over_rep(lambda rr: l_rep(rr, rep).wait_send())
+    finish(oz_r, ZN - 1, oz_recv)
+    total = own[z]
+    for t in range(1, ZN):
+        total += oz_r[lax.rem(z + t, ZN)].astype(F32)
+    qgrad_ref[...] = total
 
 
 def on_device(G, R, queries, passages, lengths, cand_ids, owner_map, teacher, weights):
@@ -561,7 +580,6 @@
     pitch = -(-token_len // 8) * 8
     ZN = G // YN
     vmem = pl.BlockSpec(memory_space=pltpu.VMEM)
-    smem = pl.BlockSpec(memory_space=pltpu.SMEM)
     hbm = pl.BlockSpec(memory_space=pl.ANY)
     dma = pltpu.SemaphoreType.DMA
     loss, qgrad, pgrad = pl.pallas_call(
@@ -571,9 +589,15 @@
             pltpu.VMEM((query_local, query_len, dim), F32),
             pltpu.VMEM((token_len, stored, dim), BF16),
         ),
-        in_specs=[vmem, vmem, vmem, hbm, smem, vmem, smem],
+        in_specs=[hbm] * 7,
         out_specs=(vmem, vmem, vmem),
         scratch_shapes=[
+            pltpu.VMEM(cand_ids.shape, I32),
+            pltpu.VMEM(owner_map.shape, I32),
+            pltpu.VMEM((query_local, query_len, dim), BF16),
+            pltpu.SMEM((1, stored), I32),
+            pltpu.VMEM(teacher.shape, F32),
+            pltpu.SMEM((1, query_local), F32),
             pltpu.VMEM((token_len, stored, dim), BF16),
             pltpu.VMEM((stored * pitch, dim), F32),
             pltpu.VMEM((stored, token_len, dim), BF16),
@@ -599,14 +623,14 @@
             pltpu.VMEM((ZN, query_local, query_len, dim), BF16),
             pltpu.VMEM((ZN, query_local, query_len, dim), BF16),
             pltpu.VMEM((ZN, query_local, query_len, dim), F32),
+            pltpu.VMEM((NCH, token_len, dim), BF16),
             pltpu.VMEM((token_len, dim), F32),
+            dma((6,)),
             dma,
             dma,
         ]
-        + [dma((G,))] * 8
-        + [dma((ZN,))] * 8
-        + [dma((YN,))] * 2
-        + [dma((R,))] * 4,
+        + [dma] * 16
+        + [dma((ZN,))] * 3,
         compiler_params=pltpu.CompilerParams(
             collective_id=0, has_side_effects=True, vmem_limit_bytes=56 * 1024 * 1024
         ),

time: 57.6 us -> 52.7 us (0.915)
  Pallas kernels: 53.5 us -> 48.5 us
    pallas_call x1, Pallas kernels: 53.5 us -> 48.5 us  [on_device(): pl.pallas_call(functools.partial(step_kernel, G, R, NCH), out_shape=(pltp...]
where the time goes in v5:
time: 52.7 us; the launch traced here: 52.5 us
  Pallas kernels  48.5 us (92%)
  local copies, waits for them, and re-layouts  2.22 us (4%)
  between operations  1.81 us (3%)
    pallas_call x1, Pallas kernels, on_device(): pl.pallas_call(functools.partial(step_kernel, G, R, NCH), out_shape=(pltp...  48.5 us
    unnamed x2, local copies, waits for them, and re-layouts  2.22 us

profile of v5, /device:TPU:2, one launch (start us, length us, event | category | flops | bytes accessed | tf_op | source)
XLA Modules:
  0.0 52.5 jit_solution(15198800452505833125)
XLA Ops:
  0.6 48.5 %shard_map.94 = (f32[1,128]{1,0:T(1,128)S(1)}, f32[2,32,128]{2,1,0:T(8,128)S(1)}, bf16[180,64,128]{2,1,0:T(8,128)(2,1)S(1)}) custom-call(s32[2,1,64]{2,1,0:T(1,128)} %cand_hbm.1, s32[1,2048]{1,0:T(1,128)} %omap_hbm.1, bf16[2,32,128]{2,1,0:T(8,128)(2,1)} %bitcast.18, bf16[180,64,128]{2,1,0:T(8,128)(2,1)} %bitcast.17, s32[1,64]{1,0:T(1,128)} %bitcast.19, ...), custom_call_target="tpu_custom_call" | custom-call | tf_op jit(solution)/shard_map/pallas_call | solution.py:585
  49.2 0.6 %copy.14 = f32[2,1,32,128]{3,2,1,0:T(8,128)} copy(f32[2,1,32,128]{3,2,1,0:T(8,128)S(1)} %bitcast.15) | data formatting | bytes 65536
  49.8 1.6 %copy.15 = bf16[64,1,180,128]{3,0,2,1:T(8,128)(2,1)} copy(bf16[64,1,180,128]{3,0,2,1:T(8,128)(2,1)S(1)} %bitcast.14) | data formatting | bytes 5898240

commit v6 on v5

--- a/solution.py
+++ b/solution.py
@@ -17,8 +17,7 @@
 LANES = 128
 CAP = 8
 WIDE = 4
-UNROLL = 8
-PART = 9
+UNROLL = 16
 LOW = -3e38
 YN = 4
 
@@ -70,8 +69,7 @@
     c_v,
     t_r,
     v_r,
-    gz_r,
-    gy_r,
+    g_r,
     wr,
     lr,
     meta_v,
@@ -104,8 +102,7 @@
     ty_recv,
     qy_recv,
     v_recv,
-    gz_recv,
-    gy_recv,
+    g_recv,
     oz_recv,
     w_recv,
     l_recv,
@@ -427,18 +424,13 @@
         by_slot.append(grad)
         sgq[:, k, :] = jnp.broadcast_to(jnp.where(late, 0.0, grad), (G, LANES))
         sgq[:, CAP + k, :] = jnp.broadcast_to(jnp.where(late, grad, 0.0), (G, LANES))
-    gz_r[z] = jnp.broadcast_to(jnp.sum(part, axis=0, keepdims=True), (1, LANES))
-
-    def g_z(to, src):
-        return remote(gz_r.at[src], gz_r.at[src], g_sent, gz_recv, to * YN + y, rep)
-
-    def g_y(to, src):
-        return remote(gy_r.at[src], gy_r.at[src], g_sent, gy_recv, z * YN + to, rep)
+    g_r[me] = jnp.broadcast_to(jnp.sum(part, axis=0, keepdims=True), (1, LANES))
+
+    def g_to(to):
+        return remote(g_r.at[me], g_r.at[me], g_sent, g_recv, to, rep)
 
     def l_rep(to, src):
         return remote(lr.at[src], lr.at[src], l_sent, l_recv, me, to)
-
-    over_z(lambda zz: g_z(zz, z).start())
 
     def query_sum(s):
         scales = sgq[s]
@@ -468,8 +460,14 @@
 
         over_y(one_way)
 
-    over_z(send_sums, far=True)
+    def send_sums_and_part(zz):
+        send_sums(zz)
+        for yy in range(YN):
+            g_to(zz * YN + yy).start()
+
+    over_z(send_sums_and_part, far=True)
     send_sums(z)
+    over_y(lambda yy: g_to(z * YN + yy).start())
 
     def keep_sums(zz):
         one, two = query_sum(zz * YN + y)
@@ -512,12 +510,6 @@
         acc[...] = total
         return carry
 
-    lax.fori_loop(0, min(PART, groups), back_group, 0)
-    finish(gz_r, ZN - 1, gz_recv)
-    gy_r[y] = jnp.sum(gz_r[...], axis=0)
-    over_y(lambda yy: g_y(yy, y).start())
-    lax.fori_loop(min(PART, groups), groups, back_group, 0)
-
     def line_sum(zz):
         finish(oy_r, YN - 1, oy_recv.at[zz])
         total = own[zz]
@@ -529,10 +521,18 @@
         oz_s[zz] = line_sum(zz).astype(BF16)
         o_z(zz, z).start()
 
-    over_z(send_line, far=True)
+    share = groups // (ZN - 1)
+
+    def send_between(t, carry):
+        lax.fori_loop((t - 1) * share, t * share, back_group, 0)
+        send_line(near_z(ZN - t))
+        return carry
+
+    lax.fori_loop(1, ZN, send_between, 0)
+    lax.fori_loop(share * (ZN - 1), groups, back_group, 0)
     own[z] = line_sum(z)
-    finish(gy_r, YN - 1, gy_recv)
-    lr[rep] = jnp.sum(gy_r[...], axis=0)
+    finish(g_r, G - 1, g_recv)
+    lr[rep] = jnp.sum(g_r[...], axis=0)
     over_rep(lambda rr: l_rep(rr, rep).start())
 
     def place(i, carry):
@@ -556,7 +556,7 @@
     finish(t_r, G - 1, t_sent)
     finish(q_all, 2 * (G - 1), q_sent)
     finish(v_r, G - 1, v_sent)
-    finish(v_r, ZN + YN - 2, g_sent)
+    finish(g_r, G - 1, g_sent)
     finish(oy_s, ZN * (YN - 1), oy_sent)
     finish(oz_s, ZN - 1, oz_sent)
     finish(wr, R - 1, w_sent)
@@ -605,8 +605,7 @@
             pltpu.VMEM((1, LANES), I32),
             pltpu.VMEM((G, 3, LANES), F32),
             pltpu.VMEM((G, 1, LANES), F32),
-            pltpu.VMEM((ZN, 1, LANES), F32),
-            pltpu.VMEM((YN, 1, LANES), F32),
+            pltpu.VMEM((G, 1, LANES), F32),
             pltpu.VMEM((R, 1, LANES), F32),
             pltpu.VMEM((R, 1, LANES), F32),
             pltpu.VMEM((8, LANES), I32),
@@ -629,7 +628,7 @@
             dma,
             dma,
         ]
-        + [dma] * 16
+        + [dma] * 15
         + [dma((ZN,))] * 3,
         compiler_params=pltpu.CompilerParams(
             collective_id=0, has_side_effects=True, vmem_limit_bytes=56 * 1024 * 1024

time: 52.7 us -> 49.6 us (0.941)
  Pallas kernels: 48.5 us -> 45.4 us
    pallas_call x1, Pallas kernels: 48.5 us -> 45.4 us  [on_device(): pl.pallas_call(functools.partial(step_kernel, G, R, NCH), out_shape=(pltp...]
where the time goes in v6:
time: 49.6 us; the launch traced here: 49.4 us
  Pallas kernels  45.4 us (92%)
  local copies, waits for them, and re-layouts  2.22 us (4%)
  between operations  1.81 us (4%)
    pallas_call x1, Pallas kernels, on_device(): pl.pallas_call(functools.partial(step_kernel, G, R, NCH), out_shape=(pltp...  45.4 us
    unnamed x2, local copies, waits for them, and re-layouts  2.22 us

profile of v6, /device:TPU:2, one launch (start us, length us, event | category | flops | bytes accessed | tf_op | source)
XLA Modules:
  0.0 49.4 jit_solution(15751623342760946312)
XLA Ops:
  0.6 45.4 %shard_map.94 = (f32[1,128]{1,0:T(1,128)S(1)}, f32[2,32,128]{2,1,0:T(8,128)S(1)}, bf16[180,64,128]{2,1,0:T(8,128)(2,1)S(1)}) custom-call(s32[2,1,64]{2,1,0:T(1,128)} %cand_hbm.1, s32[1,2048]{1,0:T(1,128)} %omap_hbm.1, bf16[2,32,128]{2,1,0:T(8,128)(2,1)} %bitcast.18, bf16[180,64,128]{2,1,0:T(8,128)(2,1)} %bitcast.17, s32[1,64]{1,0:T(1,128)} %bitcast.19, ...), custom_call_target="tpu_custom_call" | custom-call | tf_op jit(solution)/shard_map/pallas_call | solution.py:585
  46.0 0.6 %copy.14 = f32[2,1,32,128]{3,2,1,0:T(8,128)} copy(f32[2,1,32,128]{3,2,1,0:T(8,128)S(1)} %bitcast.15) | data formatting | bytes 65536
  46.6 1.6 %copy.15 = bf16[64,1,180,128]{3,0,2,1:T(8,128)(2,1)} copy(bf16[64,1,180,128]{3,0,2,1:T(8,128)(2,1)S(1)} %bitcast.14) | data formatting | bytes 5898240

commit v7 on v6

--- a/solution.py
+++ b/solution.py
@@ -18,6 +18,7 @@
 CAP = 8
 WIDE = 4
 UNROLL = 16
+FWD, LIFT = 56, 28
 LOW = -3e38
 YN = 4
 
@@ -137,11 +138,9 @@
         return lax.rem(z + odd * ((t + 1) // 2) + (1 - odd) * (ZN - t // 2), ZN)
 
     def over_z(body, far=False):
-        def one(t, carry):
-            body(near_z(ZN - t if far else t))
-            return carry
-
-        lax.fori_loop(1, ZN, one, 0)
+        for t in range(1, ZN):
+            t = ZN - t if far else t
+            body(lax.rem(z + ((t + 1) // 2 if t % 2 else ZN - t // 2), ZN))
 
     def over_y(body):
         for t in range(1, YN):
@@ -226,12 +225,12 @@
     pitch = p_f.shape[0] // stored
 
     def spread(i, carry):
-        for u in range(4):
-            j = i * 4 + u
+        for u in range(12):
+            j = i * 12 + u
             p_f[pl.ds(j, stored, stride=pitch), :] = pt_v[j].astype(F32)
         return carry
 
-    lax.fori_loop(0, token_len // 4, spread, 0)
+    lax.fori_loop(0, token_len // 12, spread, 0)
 
     def settle(t):
         for u in range(stored // ZN):
@@ -336,11 +335,11 @@
         return highest + temper * jnp.log(summed)
 
     def forward_group(g, carry):
-        rows = [forward(g * UNROLL + u) for u in range(UNROLL)]
-        m_v[pl.ds(pl.multiple_of(g * UNROLL, UNROLL), UNROLL), :] = jnp.concatenate(rows, axis=0)
-        return carry
-
-    lax.fori_loop(0, NCH // UNROLL, forward_group, 0)
+        rows = [forward(g * FWD + u) for u in range(FWD)]
+        m_v[pl.ds(pl.multiple_of(g * FWD, FWD), FWD), :] = jnp.concatenate(rows, axis=0)
+        return carry
+
+    lax.fori_loop(0, NCH // FWD, forward_group, 0)
 
     matched = m_v[...]
     block = iota((LANES, LANES), 1) >> 5
@@ -382,12 +381,12 @@
         u_v[pl.ds(ch * WIDE, WIDE)] = u.astype(BF16).reshape(WIDE, query_len, dim)
 
     def lift_group(g, carry):
-        for u in range(UNROLL):
-            lift(g * UNROLL + u)
+        for u in range(LIFT):
+            lift(g * LIFT + u)
         return carry
 
     groups = NCH // UNROLL
-    lax.fori_loop(0, groups, lift_group, 0)
+    lax.fori_loop(0, NCH // LIFT, lift_group, 0)
 
     teacher = t_r[:, 0, :]
     half = ylane >> 6
@@ -536,22 +535,22 @@
     over_rep(lambda rr: l_rep(rr, rep).start())
 
     def place(i, carry):
-        for u in range(4):
-            p = i * 4 + u
+        for u in range(8):
+            p = i * 8 + u
             mark = meta_s[6, p]
             rows = sums[jnp.maximum(mark - 1, 0)].astype(F32) * jnp.where(mark > 0, 1.0, 0.0)
             p_f[pl.ds(p, token_len, stride=stored), :] = rows
         return carry
 
-    lax.fori_loop(0, stored // 4, place, 0)
+    lax.fori_loop(0, stored // 8, place, 0)
 
     def pack(i, carry):
-        for u in range(4):
-            j = i * 4 + u
+        for u in range(12):
+            j = i * 12 + u
             pgrad_ref[j] = p_f[pl.ds(pl.multiple_of(j * stored, stored), stored), :].astype(BF16)
         return carry
 
-    lax.fori_loop(0, token_len // 4, pack, 0)
+    lax.fori_loop(0, token_len // 12, pack, 0)
 
     finish(t_r, G - 1, t_sent)
     finish(q_all, 2 * (G - 1), q_sent)

time: 49.6 us -> 48.6 us (0.980)
  Pallas kernels: 45.4 us -> 44.5 us
    pallas_call x1, Pallas kernels: 45.4 us -> 44.5 us  [on_device(): pl.pallas_call(functools.partial(step_kernel, G, R, NCH), out_shape=(pltp...]
where the time goes in v7:
time: 48.6 us; the launch traced here: 48.5 us
  Pallas kernels  44.5 us (92%)
  local copies, waits for them, and re-layouts  2.22 us (5%)
  between operations  1.81 us (4%)
    pallas_call x1, Pallas kernels, on_device(): pl.pallas_call(functools.partial(step_kernel, G, R, NCH), out_shape=(pltp...  44.5 us
    unnamed x2, local copies, waits for them, and re-layouts  2.22 us

profile of v7, /device:TPU:2, one launch (start us, length us, event | category | flops | bytes accessed | tf_op | source)
XLA Modules:
  0.0 48.5 jit_solution(17970068713777226634)
XLA Ops:
  0.6 44.5 %shard_map.94 = (f32[1,128]{1,0:T(1,128)S(1)}, f32[2,32,128]{2,1,0:T(8,128)S(1)}, bf16[180,64,128]{2,1,0:T(8,128)(2,1)S(1)}) custom-call(s32[2,1,64]{2,1,0:T(1,128)} %cand_hbm.1, s32[1,2048]{1,0:T(1,128)} %omap_hbm.1, bf16[2,32,128]{2,1,0:T(8,128)(2,1)} %bitcast.18, bf16[180,64,128]{2,1,0:T(8,128)(2,1)} %bitcast.17, s32[1,64]{1,0:T(1,128)} %bitcast.19, ...), custom_call_target="tpu_custom_call" | custom-call | tf_op jit(solution)/shard_map/pallas_call | solution.py:584
  45.1 0.6 %copy.14 = f32[2,1,32,128]{3,2,1,0:T(8,128)} copy(f32[2,1,32,128]{3,2,1,0:T(8,128)S(1)} %bitcast.15) | data formatting | bytes 65536
  45.7 1.6 %copy.15 = bf16[64,1,180,128]{3,0,2,1:T(8,128)(2,1)} copy(bf16[64,1,180,128]{3,0,2,1:T(8,128)(2,1)S(1)} %bitcast.14) | data formatting | bytes 5898240
